TPU v7x, 128 devices: a whole 4x4x4 slice. The times are simulated.
128 devices in a mesh: band: 16 (over z, x), coef: 8 (over y, core).
Axes of the slice: x: 4, y: 4, z: 4, core: 2. Of those that a mesh axis runs over, the one named last changes fastest.
Arguments:
- coeffs: float32 [1024, 262144], P('band', 'coef'), may hold values from -320 to 320
- ref_block: float32 [1024, 262144], P('band', 'coef'), may hold values from -0.01171875 to 0.01171875
- index_map: int32 [262144], P('coef'), may hold values from 0 to 32767, as said below
- band_group: int32 [1024], P('band'), may hold values from 0 to 15
Outputs:
- ortho: float32 [1024, 262144], P('band', 'coef')
- band_residual: float32 [1024], P('band')
- group_residual: float32 [16], replicated
Inputs may be any that keep to these rules, and one draw needn't show every extreme that they name: Within each aligned slab of 32768 coefficients, index_map holds every number of 0 to 32767 once.
All inputs are finite; a program needn't handle non-finite values.
Results may differ from a plain program's by a relative error of at most 0.000098.
Values sent between devices are 32-bit elements; how exact they have to be, the bound alone decides.
A program may use at most 192 MiB of HBM per device.

v0:
```python
import jax
import jax.numpy as jnp
from jax import lax
from jax.sharding import PartitionSpec as P

NB = 1024
NGROUPS = 16


def copy_for_each(x, axis):
    copies = jnp.broadcast_to(x, (lax.axis_size(axis), *x.shape))
    return lax.all_to_all(copies, axis, split_axis=0, concat_axis=0, tiled=True)


def of_everyone(x, axis):
    return copy_for_each(x, axis).sum(axis=0)


def local(coeffs, ref_block, index_map, band_group):
    columns = lax.all_to_all(coeffs, "band", split_axis=1, concat_axis=0, tiled=True)
    partial_value = jnp.dot(
        columns, columns.T, precision=lax.Precision.HIGHEST, preferred_element_type=jnp.float32
    )
    margin = lax.psum(partial_value, ("band", "coef"))
    factor = jnp.linalg.cholesky(margin)
    ortho_cols = lax.linalg.triangular_solve(factor, columns, left_side=True, lower=True)
    ortho = lax.all_to_all(ortho_cols, "band", split_axis=0, concat_axis=1, tiled=True)
    aligned = jnp.take(ortho, index_map, axis=1)
    squares = jnp.sum((aligned - ref_block) ** 2, axis=1)
    group_range = jnp.arange(NGROUPS, dtype=jnp.int32)
    totals = of_everyone(squares, "coef")
    band_residual = jnp.sqrt(totals + 1e-06)
    onehot = (band_group[:, None] == group_range[None, :]).astype(jnp.float32)
    terms = jnp.dot(
        band_residual, onehot, precision=lax.Precision.HIGHEST, preferred_element_type=jnp.float32
    )
    group_residual = of_everyone(terms, "band") * (NGROUPS / NB)
    return (ortho, band_residual, group_residual)


def solution(mesh):
    return jax.shard_map(
        local,
        mesh=mesh,
        in_specs=(P("band", "coef"), P("band", "coef"), P("coef"), P("band")),
        out_specs=(P("band", "coef"), P("band"), P()),
        check_vma=False,
    )
```

profile of v0, /device:TPU:1, one launch (start us, length us, event | category | flops | bytes accessed | tf_op | source)
XLA Modules:
  0.0 988.4 jit_solution(1587776855697686987)
XLA Ops:
  7.2 4.0 copy.54
  11.2 102.9 %all_to_all.50 = f32[64,16,2048]{2,0,1:T(8,128)S(1)} all-to-all(f32[64,16,2048]{2,0,1:T(8,128)S(1)} %bitcast.139), channel_id=1, replica_groups=mesh['band'=16,'coef'=8] {'band'}, dimensions={1} | all-to-all | bytes 16777216 | tf_op jit(solution)/shard_map/all_to_all | solution.py:20
  114.1 3.4 copy-done
  117.5 28.8 %fusion.75 = f32[1024,1024]{0,1:T(8,128)} fusion(f32[1024,2048]{1,0:T(8,128)S(1)} %bitcast.137), kind=kOutput, calls=%fused_computation.171 | convolution fusion | flops 25769803776 | bytes 12582912 | tf_op jit(solution)/shard_map/dot_general | solution.py:21
  146.3 5.9 fusion.74
  152.2 147.5 %all-reduce.3.cloned.1.call-done = f32[1024,1024]{0,1:T(8,128)} async-done(((f32[1024,1024]{0,1:T(8,128)}), f32[1024,1024]{0,1:T(8,128)}) %all-reduce.3.cloned.1.call-update) | async-done | bytes 4194320 | tf_op jit(solution)/shard_map/psum | solution.py:24
  299.8 5.3 copy.45
  305.1 4.4 fusion.10
  311.5 11.7 %cholesky.223 = f32[128,128]{1,0:T(8,128)S(1)} custom-call(f32[128,128]{1,0:T(8,128)S(1)} %cholesky.580), custom_call_target="Cholesky" | custom-call | tf_op jit(solution)/shard_map/jit(cholesky)/cholesky | solution.py:25
  323.2 9.8 custom-call.62
  340.2 11.9 %cholesky.244 = f32[128,128]{1,0:T(8,128)S(1)} custom-call(f32[128,128]{1,0:T(8,128)S(1)} %cholesky.584), custom_call_target="Cholesky" | custom-call | tf_op jit(solution)/shard_map/jit(cholesky)/cholesky | solution.py:25
  352.7 9.8 custom-call.63
  367.5 13.2 %cholesky.468 = f32[128,128]{1,0:T(8,128)} custom-call(f32[128,128]{1,0:T(8,128)} %cholesky.589), custom_call_target="Cholesky" | custom-call | tf_op jit(solution)/shard_map/jit(cholesky)/cholesky | solution.py:25
  382.8 11.3 %custom-call.64 = f32[1,128,128]{1,2,0:T(8,128)} custom-call(f32[1,128,128]{2,1,0:T(8,128)} %get-tuple-element.87), custom_call_target="InvertDiagBlocksLowerTriangular" | custom-call | tf_op jit(solution)/shard_map/jit(cholesky)/cholesky | solution.py:25
  398.4 12.5 %cholesky.487 = f32[128,128]{1,0:T(8,128)} custom-call(f32[128,128]{1,0:T(8,128)S(1)} %cholesky.594), custom_call_target="Cholesky" | custom-call | tf_op jit(solution)/shard_map/jit(cholesky)/cholesky | solution.py:25
  413.1 10.4 %custom-call.65 = f32[1,128,128]{1,2,0:T(8,128)} custom-call(f32[1,128,128]{2,1,0:T(8,128)S(1)} %get-tuple-element.84), custom_call_target="InvertDiagBlocksLowerTriangular" | custom-call | tf_op jit(solution)/shard_map/jit(cholesky)/cholesky | solution.py:25
  427.8 11.7 %cholesky.506 = f32[128,128]{1,0:T(8,128)S(1)} custom-call(f32[128,128]{1,0:T(8,128)S(1)} %cholesky.599), custom_call_target="Cholesky" | custom-call | tf_op jit(solution)/shard_map/jit(cholesky)/cholesky | solution.py:25
  440.8 10.2 %custom-call.66 = f32[1,128,128]{1,2,0:T(8,128)S(1)} custom-call(f32[1,128,128]{2,1,0:T(8,128)S(1)} %get-tuple-element.81), custom_call_target="InvertDiagBlocksLowerTriangular" | custom-call | tf_op jit(solution)/shard_map/jit(cholesky)/cholesky | solution.py:25
  454.3 11.7 %cholesky.526 = f32[128,128]{1,0:T(8,128)S(1)} custom-call(f32[128,128]{1,0:T(8,128)S(1)} %cholesky.604), custom_call_target="Cholesky" | custom-call | tf_op jit(solution)/shard_map/jit(cholesky)/cholesky | solution.py:25
  467.3 9.8 custom-call.67
  480.1 11.8 %cholesky.546 = f32[128,128]{1,0:T(8,128)S(1)} custom-call(f32[128,128]{1,0:T(8,128)S(1)} %cholesky.609), custom_call_target="Cholesky" | custom-call | tf_op jit(solution)/shard_map/jit(cholesky)/cholesky | solution.py:25
  493.2 9.8 custom-call.68
  505.7 11.7 %cholesky.564 = f32[128,128]{1,0:T(8,128)S(1)} custom-call(f32[128,128]{1,0:T(8,128)S(1)} %convolution_subtract_fusion.11), custom_call_target="Cholesky" | custom-call | tf_op jit(solution)/shard_map/jit(cholesky)/cholesky | solution.py:25
  524.2 4.9 select_select_fusion
  529.1 28.9 %while.1 = (s32[]{:T(128)}, f32[1024,1024]{1,0:T(8,128)}, s32[8,2]{0,1:T(2,128)S(1)}, f32[8,128,128]{2,1,0:T(8,128)}, s32[]{:T(128)}) while((s32[]{:T(128)}, f32[1024,1024]{1,0:T(8,128)}, s32[8,2]{0,1:T(2,128)S(1)}, f32[8,128,128]{2,1,0:T(8,128)}, s32[]{:T(128)}) %tuple.74), condition=%wide.while_cond, body=%wide.while_body.sunk | while | flops 2 | bytes 132705 | solution.py:26
  529.8 3.0 bitcast_dynamic-update-slice_fusion.2
  533.4 3.0 bitcast_dynamic-update-slice_fusion.2
  537.0 3.0 bitcast_dynamic-update-slice_fusion.2
  540.6 3.0 bitcast_dynamic-update-slice_fusion.2
  544.3 3.0 bitcast_dynamic-update-slice_fusion.2
  547.9 3.0 bitcast_dynamic-update-slice_fusion.2
  551.5 2.9 bitcast_dynamic-update-slice_fusion.2
  558.0 80.2 %custom-call.69 = f32[8,128,128]{1,2,0:T(8,128)} custom-call(f32[8,128,128]{2,1,0:T(8,128)} %get-tuple-element.10), custom_call_target="InvertDiagBlocksLowerTriangular" | custom-call | tf_op jit(solution)/shard_map/triangular_solve | solution.py:26
  647.5 3.0 fusion.17
  651.8 3.3 fusion.20
  656.7 4.1 convolution_subtract_fusion.2
  662.0 4.4 convolution_subtract_fusion
  667.5 5.4 convolution_subtract_fusion.1
  674.0 3.4 copy-done.1
  677.4 5.5 all-to-all-start.1
  682.9 12.2 %copy.47 = f32[64,32768]{0,1:T(8,128)} copy(f32[64,32768]{1,0:T(8,128)} %param.5) | data formatting | bytes 16777216 | tf_op args[1]
  695.3 112.0 %all-to-all-done.1 = f32[16,64,2048]{2,1,0:T(8,128)} async-done(((f32[16,64,2048]{2,1,0:T(8,128)}), f32[16,64,2048]{2,1,0:T(8,128)}, u32[]{:S(2)}, u32[]{:S(2)}) %all-to-all-start.1) | async-done | bytes 8388640 | tf_op jit(solution)/shard_map/all_to_all | solution.py:27
  807.2 12.2 %copy.46 = f32[64,16,2048]{0,2,1:T(8,128)} copy(f32[64,16,2048]{2,0,1:T(8,128)} %bitcast.34) | data formatting | bytes 16777216 | tf_op jit(solution)/shard_map/all_to_all | solution.py:27
  819.4 114.0 %gather_fusion = f32[32768,64]{1,0:T(8,128)} fusion(f32[64,32768]{0,1:T(8,128)} %bitcast.135, s32[32768]{0:T(1024)S(1)} %fusion.50), kind=kCustom, calls=%fused_computation | custom fusion | bytes 16908288 | tf_op jit(solution)/shard_map/jit(_take)/gather | solution.py:28
  933.5 18.5 %fusion.1 = f32[64]{0:T(128)S(1)} fusion(f32[64,32768]{0,1:T(8,128)} %copy.47, f32[32768,64]{1,0:T(8,128)} %gather_fusion, pred[32768]{0:T(1024)(128)(4,1)S(1)} %compare_and_fusion), kind=kLoop, calls=%fused_computation.5 | loop fusion | flops 8388544 | bytes 16810240 | tf_op jit(solution)/shard_map/reduce_sum | solution.py:29
  952.0 11.8 %all_to_all.51 = f32[8,1,64]{2,1,0:T(1,128)S(1)} all-to-all(f32[8,1,64]{2,1,0:T(1,128)S(1)} %broadcast_in_dim.25), channel_id=1, replica_groups=mesh['band'=16,'coef'=8] {'coef'}, dimensions={0} | all-to-all | bytes 4096 | tf_op jit(solution)/shard_map/all_to_all | solution.py:12
  964.7 3.4 all-to-all-start.3
  968.1 12.7 %copy.50 = f32[64,32768]{1,0:T(8,128)} copy(f32[64,32768]{0,1:T(8,128)} %bitcast.136) | data formatting | bytes 16777216
  (101 shorter events, 67.3 us)
Async XLA Ops:
  7.2 292.6 %all-reduce.3.cloned.1.call-start = ((), (), s32[]{:S(2)}) async-start(), calls=%async_computation.4 | async-start | bytes 8388608 | tf_op jit(solution)/shard_map/psum | solution.py:24
  114.1 3.4 copy-start
  309.5 1.9 copy-start.2
  339.4 0.8 copy-start.6
  638.2 4.5 copy-start.8
  640.8 3.2 copy-start.4
  646.3 1.3 copy-start.3
  650.5 1.3 copy-start.7
  655.1 1.6 copy-start.5
  674.0 3.4 copy-start.1
  677.4 129.8 %all-to-all-start.1 = ((f32[16,64,2048]{2,1,0:T(8,128)}), f32[16,64,2048]{2,1,0:T(8,128)}, u32[]{:S(2)}, u32[]{:S(2)}) async-start(f32[16,64,2048]{2,1,0:T(8,128)} %bitcast.140), calls=%async_computation.1 | async-start | bytes 16777216 | tf_op jit(solution)/shard_map/all_to_all | solution.py:27
  682.9 12.3 %copy-start.9 = (s32[32768]{0:T(1024)S(1)}, s32[32768]{0:T(1024)}, u32[]{:S(2)}) copy-start(s32[32768]{0:T(1024)} %param.6) | copy-start | bytes 393220
  933.5 30.4 %copy-start.10 = (s32[64]{0:T(128)S(1)}, s32[64]{0:T(128)}, u32[]{:S(2)}) copy-start(s32[64]{0:T(128)} %param.7) | copy-start | bytes 772
  963.9 16.9 %copy-start.11 = (f32[64]{0:T(128)}, f32[64]{0:T(128)S(1)}, u32[]{:S(2)}) copy-start(f32[64]{0:T(128)S(1)} %add_sqrt_fusion) | copy-start | bytes 772
  964.7 16.1 %all-to-all-start.3 = ((f32[16,1,16]{2,1,0:T(1,128)}), f32[16,1,16]{2,1,0:T(1,128)S(1)}, u32[]{:S(2)}, u32[]{:S(2)}) async-start(f32[16,1,16]{2,1,0:T(1,128)} %broadcast_in_dim.26), calls=%async_computation.3 | async-start | bytes 16384 | tf_op jit(solution)/shard_map/all_to_all | solution.py:12
Sparse Core Ops, SparseCore 0:
  146.4 153.3 all-reduce.2
where the time goes:
time: 1000 us; the launch traced here: 988 us
  other arithmetic  287 us (29%)
  waiting for transfers between devices  260 us (26%)
  local copies, waits for them, and re-layouts  209 us (21%)
  blocking collectives  115 us (12%)
  matrix products  90.1 us (9%)
  between operations  19.6 us (2%)
    another operation x30, other arithmetic, local(): factor = jnp.linalg.cholesky(margin)  178 us
    psum x1, waiting for transfers between devices, local(): margin = lax.psum(partial_value, ('band', 'coef'))  148 us
    gather x1, local copies, waits for them, and re-layouts, local(): aligned = jnp.take(ortho, index_map, axis=1)  114 us
    all_to_all x1, waiting for transfers between devices, local(): lax.all_to_all(ortho_cols, 'band', split_axis=0, concat_axis=1, tiled=True)  112 us
    all_to_all x1, blocking collectives, local(): lax.all_to_all(coeffs, 'band', split_axis=1, concat_axis=0, tiled=True)  103 us
    another operation x3, other arithmetic, local(): lax.linalg.triangular_solve(factor, columns, left_side=True, lower=True)  85.1 us
    another operation x15, matrix products, local(): lax.linalg.triangular_solve(factor, columns, left_side=True, lower=True)  35.5 us
    unnamed x26, local copies, waits for them, and re-layouts  34.4 us
  transfers between devices with their start and end apart: 3, of which 2 were waited for; matrix products, arithmetic and copies ran while one was open for 3% of the time, Pallas kernels for 0%

commit v1 on v0

v1 whole, which is shorter than its diff:
```python
import functools
import jax
import jax.numpy as jnp
from jax import lax
from jax.experimental import pallas as pl
from jax.experimental.pallas import tpu as pltpu

BLK = 128
PAN = 8
F32 = jnp.float32
BF = jnp.bfloat16


def split(x):
    hi = x.astype(BF)
    return hi, (x - hi.astype(F32)).astype(BF)


def dot3(ah, al, bh, bl, dims):
    d = functools.partial(lax.dot_general, dimension_numbers=(dims, ((), ())), preferred_element_type=F32)
    return d(ah, bh) + (d(ah, bl) + d(al, bh))


NN = ((1,), (0,))
NT = ((1,), (1,))


def lanes_of(x, lane):
    return jnp.take_along_axis(x, jnp.full(x.shape, lane, jnp.int32), axis=1)


def row_of(x, j):
    return jnp.broadcast_to(x[j : j + 1, :], (PAN, BLK))


def rows_sum(cols, rows):
    parts = [c * r for c, r in zip(cols, rows)]
    while len(parts) > 1:
        parts = [parts[i] + parts[i + 1] for i in range(0, len(parts), 2)]
    return parts[0]


def diag_inverse(a_ref, w_ref, m_ref):
    sub = lax.broadcasted_iota(jnp.int32, (PAN, BLK), 0)
    r_i = lax.broadcasted_iota(jnp.int32, (BLK, BLK), 0)
    c_i = lax.broadcasted_iota(jnp.int32, (BLK, BLK), 1)
    w_ref[...] = (r_i == c_i).astype(F32)

    def body(p, carry):
        x, *cols = carry
        base = pl.multiple_of(p * PAN, PAN)
        nxt = pl.multiple_of(jnp.minimum(base + PAN, BLK - PAN), PAN)
        fwd = w_ref[pl.ds(base, PAN), :]
        kw = fwd
        scale = jnp.zeros((PAN, BLK), F32)
        for j in range(PAN):
            d = row_of(cols[j], j)
            r = 1.0 / d
            f = cols[j] * r
            isj = sub == j
            for m in range(j + 1, PAN):
                b = row_of(cols[m], j)
                cols[m] = jnp.where(isj, b * r, cols[m] - f * b)
            b = row_of(x, j)
            x = jnp.where(isj, b * r, x - f * b)
            b = row_of(kw, j)
            kw = jnp.where(isj, b * r, kw - f * b)
            if j < PAN - 1:
                fwd = jnp.where(sub > j, fwd - f * row_of(fwd, j), fwd)
            scale = jnp.where(isj, lax.rsqrt(d), scale)
        m_ref[pl.ds(base, PAN), :] = fwd * scale
        xb = [row_of(x, m) for m in range(PAN)]
        kb = [row_of(kw, m) for m in range(PAN)]
        an = a_ref[pl.ds(nxt, PAN), :]
        xn = an - rows_sum([lanes_of(an, base + m) for m in range(PAN)], xb)
        new_cols = [lanes_of(xn, nxt + m) for m in range(PAN)]
        for s in range(0, BLK, PAN):
            a = a_ref[s : s + PAN, :]
            am = [lanes_of(a, base + m) for m in range(PAN)]
            a_ref[s : s + PAN, :] = a - rows_sum(am, xb)
            w_ref[s : s + PAN, :] = w_ref[s : s + PAN, :] - rows_sum(am, kb)
        return (xn, *new_cols)

    x0 = a_ref[0:PAN, :]
    lax.fori_loop(0, BLK // PAN, body, (x0, *[lanes_of(x0, m) for m in range(PAN)]))


def solve_kernel(g_ref, c_ref, y_ref, a_ref, w_ref, m_ref, lh_ref, ll_ref, yh_ref, yl_ref):
    n = g_ref.shape[0]
    for k in range(n // BLK):
        lo, hi = k * BLK, (k + 1) * BLK
        s = g_ref[lo:, lo:hi]
        if k:
            s = s - dot3(lh_ref[lo:, :lo], ll_ref[lo:, :lo], lh_ref[lo:hi, :lo], ll_ref[lo:hi, :lo], NT)
        a_ref[...] = s[:BLK]
        diag_inverse(a_ref, w_ref, m_ref)
        mh, ml = split(m_ref[...])
        if hi < n:
            sh, sl = split(s[BLK:])
            lkh, lkl = split(dot3(sh, sl, mh, ml, NT))
            lh_ref[hi:, lo:hi] = lkh
            ll_ref[hi:, lo:hi] = lkl
        z = c_ref[lo:hi, :]
        if k:
            z = z - dot3(lh_ref[lo:hi, :lo], ll_ref[lo:hi, :lo], yh_ref[:lo, :], yl_ref[:lo, :], NN)
        zh, zl = split(z)
        y = dot3(mh, ml, zh, zl, NN)
        y_ref[lo:hi, :] = y
        if hi < n:
            yh, yl = split(y)
            yh_ref[lo:hi, :] = yh
            yl_ref[lo:hi, :] = yl


def solve(g, c):
    n, w = c.shape
    return pl.pallas_call(
        solve_kernel,
        out_shape=jax.ShapeDtypeStruct((n, w), F32),
        in_specs=[pl.BlockSpec(memory_space=pltpu.VMEM)] * 2,
        out_specs=pl.BlockSpec(memory_space=pltpu.VMEM),
        scratch_shapes=[pltpu.VMEM((BLK, BLK), F32)] * 3
        + [pltpu.VMEM((n, n), BF)] * 2
        + [pltpu.VMEM((n, w), BF)] * 2,
        compiler_params=pltpu.CompilerParams(vmem_limit_bytes=60 * 2**20),
        name="solve",
    )(g, c)


def gram_kernel(c_ref, g_ref, h_ref, l_ref):
    n = c_ref.shape[0]
    b = 256
    for i in range(n // b):
        h, l = split(c_ref[i * b : (i + 1) * b, :])
        h_ref[i * b : (i + 1) * b, :] = h
        l_ref[i * b : (i + 1) * b, :] = l
        e = (i + 1) * b
        g_ref[i * b : e, :e] = dot3(h, l, h_ref[:e, :], l_ref[:e, :], NT)
        if e < n:
            g_ref[i * b : e, e:] = jnp.zeros((b, n - e), F32)


def gram(c):
    n, w = c.shape
    return pl.pallas_call(
        gram_kernel,
        out_shape=jax.ShapeDtypeStruct((n, n), F32),
        in_specs=[pl.BlockSpec(memory_space=pltpu.VMEM)],
        out_specs=pl.BlockSpec(memory_space=pltpu.VMEM),
        scratch_shapes=[pltpu.VMEM((n, w), BF)] * 2,
        compiler_params=pltpu.CompilerParams(vmem_limit_bytes=60 * 2**20),
        name="gram",
    )(c)


CH = 2048


def scatter_kernel(idx_ref, r_ref, o_ref):
    def body(i, _):
        base = i * 16
        for u in range(16):
            o_ref[pl.ds(idx_ref[base + u], 1), :] = r_ref[pl.ds(base + u, 1), :]
        return 0

    lax.fori_loop(0, CH // 16, body, 0)


def scatter_rows(idx, rows):
    n, w = rows.shape
    return pl.pallas_call(
        scatter_kernel,
        grid=(n // CH,),
        out_shape=jax.ShapeDtypeStruct((n, w), F32),
        in_specs=[
            pl.BlockSpec((CH,), lambda i: (i,), memory_space=pltpu.SMEM),
            pl.BlockSpec((CH, w), lambda i: (i, 0)),
        ],
        out_specs=pl.BlockSpec((n, w), lambda i: (0, 0)),
        compiler_params=pltpu.CompilerParams(vmem_limit_bytes=60 * 2**20),
        name="scatter",
    )(idx, rows)


from jax.sharding import PartitionSpec as P

NB = 1024
NGROUPS = 16


def copy_for_each(x, axis):
    copies = jnp.broadcast_to(x, (lax.axis_size(axis), *x.shape))
    return lax.all_to_all(copies, axis, split_axis=0, concat_axis=0, tiled=True)


def of_everyone(x, axis):
    return copy_for_each(x, axis).sum(axis=0)


def local(coeffs, ref_block, index_map, band_group):
    bands, width = coeffs.shape
    parts = lax.axis_size("band")
    part = width // parts
    blocks = coeffs.reshape(bands, parts, part).transpose(1, 0, 2)
    columns = lax.all_to_all(blocks, "band", split_axis=0, concat_axis=0, tiled=True)
    columns = columns.reshape(parts * bands, part)
    moved = scatter_rows(index_map, ref_block.T).T
    margin = lax.psum(gram(columns), ("band", "coef"))
    ortho_cols = solve(margin, columns).reshape(parts, bands, part)
    back = lax.all_to_all(ortho_cols, "band", split_axis=0, concat_axis=0, tiled=True)
    ortho = back.transpose(1, 0, 2).reshape(bands, width)
    squares = jnp.sum((ortho - moved) ** 2, axis=1)
    group_range = jnp.arange(NGROUPS, dtype=jnp.int32)
    totals = of_everyone(squares, "coef")
    band_residual = jnp.sqrt(totals + 1e-06)
    onehot = (band_group[:, None] == group_range[None, :]).astype(F32)
    terms = jnp.dot(
        band_residual, onehot, precision=lax.Precision.HIGHEST, preferred_element_type=F32
    )
    group_residual = of_everyone(terms, "band") * (NGROUPS / NB)
    return (ortho, band_residual, group_residual)


def solution(mesh):
    return jax.shard_map(
        local,
        mesh=mesh,
        in_specs=(P("band", "coef"), P("band", "coef"), P("coef"), P("band")),
        out_specs=(P("band", "coef"), P("band"), P()),
        check_vma=False,
    )
```

time: 1000 us -> 559 us (0.56); the launches traced: 988 us -> 558 us
  other arithmetic: 287 us -> 12.5 us
  local copies, waits for them, and re-layouts: 209 us -> 41.7 us
  Pallas kernels: 0 us -> 143 us
  matrix products: 90.1 us -> 0.19 us
  waiting for transfers between devices: 260 us -> 223 us
    another operation x33 -> x0, other arithmetic: 263 us -> none  [the longest x30 178 us: local(): factor = jnp.linalg.cholesky(margin)]
    pallas_call x0 -> x3, Pallas kernels: none -> 143 us  [the longest x1 86 us: solve(): pl.pallas_call(solve_kernel, out_shape=jax.ShapeDtypeStruct((n, w), F32),...]
    gather x1 -> x0, local copies, waits for them, and re-layouts: 114 us -> none  [local(): aligned = jnp.take(ortho, index_map, axis=1)]
    another operation x29 -> x0, matrix products: 61.1 us -> none  [the longest x15 35.5 us: local(): lax.linalg.triangular_solve(factor, columns, left_side=True, lower=True)]
    all_to_all x1, waiting for transfers between devices: 112 us -> 69 us  [local(): lax.all_to_all(ortho_cols, 'band', split_axis=0, concat_axis=0, tiled=True)]
    another operation x34 -> x0, local copies, waits for them, and re-layouts: 38.1 us -> none
    dot_general x1 -> x0, matrix products: 28.8 us -> none  [local(): jnp.dot(columns, columns.T, precision=lax.Precision.HIGHEST, preferred_el...]
    all_to_all x2 -> x0, local copies, waits for them, and re-layouts: 16.2 us -> none  [the longest x1 12.2 us: local(): lax.all_to_all(ortho_cols, 'band', split_axis=0, concat_axis=1, tiled=True)]
  transfers between devices with their start and end apart: 3 -> 3, of which waited for: 2 -> 2; matrix products, arithmetic and copies ran while one was open for 3% -> 4% of each run, Pallas kernels for 0% -> 8%
where the time goes in v1:
time: 559 us; the launch traced here: 558 us
  waiting for transfers between devices  223 us (40%)
  Pallas kernels  143 us (26%)
  blocking collectives  115 us (21%)
  local copies, waits for them, and re-layouts  41.7 us (7%)
  between operations  14.1 us (3%)
  other arithmetic  12.5 us (2%)
  starting transfers between devices  9.17 us (2%)
    psum x1, waiting for transfers between devices, local(): margin = lax.psum(gram(columns), ('band', 'coef'))  153 us
    all_to_all x1, blocking collectives, local(): lax.all_to_all(blocks, 'band', split_axis=0, concat_axis=0, tiled=True)  103 us
    pallas_call x1, Pallas kernels, solve(): pl.pallas_call(solve_kernel, out_shape=jax.ShapeDtypeStruct((n, w), F32),...  86 us
    all_to_all x1, waiting for transfers between devices, local(): lax.all_to_all(ortho_cols, 'band', split_axis=0, concat_axis=0, tiled=True)  69 us
    pallas_call x1, Pallas kernels, scatter_rows(): pl.pallas_call(scatter_kernel, grid=(n // CH,), out_shape=jax.ShapeDtypeS...  42.9 us
    unnamed x6, local copies, waits for them, and re-layouts  24.9 us
    pallas_call x1, Pallas kernels, gram(): pl.pallas_call(gram_kernel, out_shape=jax.ShapeDtypeStruct((n, n), F32),...  13.7 us
    transpose x1, local copies, waits for them, and re-layouts, local(): ortho = back.transpose(1, 0, 2).reshape(bands, width)  12.2 us
  transfers between devices with their start and end apart: 3, of which 2 were waited for; matrix products, arithmetic and copies ran while one was open for 4% of the time, Pallas kernels for 8%

profile of v1, /device:TPU:1, one launch (start us, length us, event | category | flops | bytes accessed | tf_op | source)
XLA Modules:
  0.0 557.7 jit_solution(4293670285044941555)
XLA Ops:
  7.2 0.0 all-reduce.2.cloned.1.call-start
  7.2 4.0 copy.27
  11.2 103.0 %all_to_all.22 = f32[16,64,2048]{2,1,0:T(8,128)} all-to-all(f32[16,64,2048]{2,1,0:T(8,128)S(1)} %bitcast.31), channel_id=1, replica_groups=mesh['band'=16,'coef'=8] {'band'}, dimensions={0} | all-to-all | bytes 16777216 | tf_op jit(solution)/shard_map/all_to_all | solution.py:205
  114.2 13.7 %gram.1 = f32[1024,1024]{1,0:T(8,128)} custom-call(f32[1024,2048]{1,0:T(8,128)} %bitcast.27), custom_call_target="tpu_custom_call" | custom-call | tf_op jit(solution)/shard_map/gram/pallas_call | solution.py:145
  127.9 0.0 all-reduce.2.cloned.1.call-update
  127.9 153.4 %all-reduce.2.cloned.1.call-done.g_ref = f32[1024,1024]{1,0:T(8,128)} async-done(((f32[1024,1024]{1,0:T(8,128)}), f32[1024,1024]{1,0:T(8,128)}) %all-reduce.2.cloned.1.call-update) | async-done | bytes 4194320 | tf_op jit(solution)/shard_map/psum | solution.py:208
  281.4 86.0 %solve.1 = f32[1024,2048]{1,0:T(8,128)} custom-call(f32[1024,1024]{1,0:T(8,128)} %all-reduce.2.cloned.1.call-done.g_ref, f32[1024,2048]{1,0:T(8,128)} %bitcast.28), custom_call_target="tpu_custom_call" | custom-call | tf_op jit(solution)/shard_map/solve/pallas_call | solution.py:117
  367.4 5.7 %all-to-all-start.1 = ((f32[16,64,2048]{2,1,0:T(8,128)}), f32[16,64,2048]{2,1,0:T(8,128)}, u32[]{:S(2)}, u32[]{:S(2)}) async-start(f32[16,64,2048]{2,1,0:T(8,128)} %bitcast.30), calls=%async_computation.1 | async-start | bytes 16777216 | tf_op jit(solution)/shard_map/all_to_all | solution.py:210
  373.1 12.2 %copy.21 = f32[64,32768]{0,1:T(8,128)} copy(f32[64,32768]{1,0:T(8,128)} %param.5) | data formatting | bytes 16777216 | tf_op args[1]
  385.4 42.9 %scatter.1 = f32[32768,64]{1,0:T(8,128)} custom-call(s32[32768]{0:T(1024)} %idx_ref.1, f32[32768,64]{1,0:T(8,128)} %bitcast.29), custom_call_target="tpu_custom_call" | custom-call | tf_op jit(solution)/shard_map/scatter/pallas_call | solution.py:171
  428.3 69.0 %all-to-all-done.1 = f32[16,64,2048]{2,1,0:T(8,128)} async-done(((f32[16,64,2048]{2,1,0:T(8,128)}), f32[16,64,2048]{2,1,0:T(8,128)}, u32[]{:S(2)}, u32[]{:S(2)}) %all-to-all-start.1) | async-done | bytes 8388640 | tf_op jit(solution)/shard_map/all_to_all | solution.py:210
  497.4 12.2 %copy.20 = f32[64,16,2048]{0,2,1:T(8,128)} copy(f32[64,16,2048]{2,0,1:T(8,128)} %bitcast.3) | data formatting | bytes 16777216 | tf_op jit(solution)/shard_map/transpose | solution.py:211
  509.6 0.0 copy-start
  509.6 12.0 %fusion.1 = f32[64]{0:T(128)S(1)} fusion(f32[32768,64]{1,0:T(8,128)} %scatter.1, f32[64,16,2048]{0,2,1:T(8,128)} %copy.20), kind=kLoop, calls=%fused_computation.2 | loop fusion | flops 6291392 | bytes 16777472 | tf_op jit(solution)/shard_map/reduce_sum | solution.py:212
  521.5 11.9 %all_to_all.23 = f32[8,1,64]{2,1,0:T(1,128)S(1)} all-to-all(f32[8,1,64]{2,1,0:T(1,128)S(1)} %broadcast_in_dim.8), channel_id=1, replica_groups=mesh['band'=16,'coef'=8] {'coef'}, dimensions={0} | all-to-all | bytes 4096 | tf_op jit(solution)/shard_map/all_to_all | solution.py:193
  533.4 0.0 copy-done
  533.4 0.0 copy-start.1
  533.4 0.2 convolution_bitcast_fusion
  533.6 0.6 broadcast_in_dim.9
  534.3 3.4 all-to-all-start.3
  537.7 12.7 %copy.24 = f32[64,32768]{1,0:T(8,128)} copy(f32[64,32768]{0,1:T(8,128)} %bitcast.26) | data formatting | bytes 16777216
  550.4 0.0 copy-done.1
  550.4 0.0 all-to-all-done.3
  550.4 0.5 broadcast_multiply_fusion
  (4 shorter events, 0.1 us)
Async XLA Ops:
  7.2 274.2 %all-reduce.2.cloned.1.call-start = ((), (), s32[]{:S(2)}) async-start(), calls=%async_computation.4 | async-start | bytes 8388608 | tf_op jit(solution)/shard_map/psum | solution.py:208
  367.4 129.9 %all-to-all-start.1 = ((f32[16,64,2048]{2,1,0:T(8,128)}), f32[16,64,2048]{2,1,0:T(8,128)}, u32[]{:S(2)}, u32[]{:S(2)}) async-start(f32[16,64,2048]{2,1,0:T(8,128)} %bitcast.30), calls=%async_computation.1 | async-start | bytes 16777216 | tf_op jit(solution)/shard_map/all_to_all | solution.py:210
  509.6 23.9 %copy-start = (s32[64]{0:T(128)S(1)}, s32[64]{0:T(128)}, u32[]{:S(2)}) copy-start(s32[64]{0:T(128)} %param.7) | copy-start | bytes 772
  533.4 16.9 %copy-start.1 = (f32[64]{0:T(128)}, f32[64]{0:T(128)S(1)}, u32[]{:S(2)}) copy-start(f32[64]{0:T(128)S(1)} %add_sqrt_fusion) | copy-start | bytes 772
  534.3 16.1 %all-to-all-start.3 = ((f32[16,1,16]{2,1,0:T(1,128)}), f32[16,1,16]{2,1,0:T(1,128)S(1)}, u32[]{:S(2)}, u32[]{:S(2)}) async-start(f32[16,1,16]{2,1,0:T(1,128)} %broadcast_in_dim.9), calls=%async_computation.3 | async-start | bytes 16384 | tf_op jit(solution)/shard_map/all_to_all | solution.py:193
Sparse Core Ops, SparseCore 0:
  128.0 153.2 all-reduce.1

commit v2 on v1

--- a/solution.py
+++ b/solution.py
@@ -4,6 +4,7 @@
 from jax import lax
 from jax.experimental import pallas as pl
 from jax.experimental.pallas import tpu as pltpu
+from jax.sharding import PartitionSpec as P
 
 BLK = 128
 PAN = 8
@@ -85,11 +86,181 @@
     lax.fori_loop(0, BLK // PAN, body, (x0, *[lanes_of(x0, m) for m in range(PAN)]))
 
 
-def solve_kernel(g_ref, c_ref, y_ref, a_ref, w_ref, m_ref, lh_ref, ll_ref, yh_ref, yl_ref):
-    n = g_ref.shape[0]
-    for k in range(n // BLK):
+MESH = pl.DeviceIdType.MESH
+NB = 1024
+NGROUPS = 16
+NBLK = NB // BLK
+TILES = NBLK * (NBLK + 1) // 2
+ANY = pl.BlockSpec(memory_space=pl.ANY)
+
+
+def tile_row(i, j):
+    return (i * (i + 1) // 2 + j) * BLK
+
+
+def place():
+    band, coef = lax.axis_index("band"), lax.axis_index("coef")
+    return band, coef, dict(z=band // 4, x=band % 4, y=coef // 2, core=coef % 2)
+
+
+def peer_on(pos, dim, value):
+    p = dict(pos)
+    p[dim] = value
+    return (p["z"] * 4 + p["x"], p["y"] * 2 + p["core"])
+
+
+def send(src, dst, ssem, rsem, device):
+    copy = pltpu.make_async_remote_copy(
+        src_ref=src, dst_ref=dst, send_sem=ssem, recv_sem=rsem, device_id=device, device_id_type=MESH
+    )
+    copy.start()
+    return copy
+
+
+ORDERS = (("z", "x", "y"), ("x", "y", "z"), ("y", "z", "x"))
+RING = 4
+HALF = TILES * BLK // 2
+PART = HALF // 3
+Q1 = PART // RING
+Q2 = Q1 // RING
+
+
+def reduce_kernel(g_ref, o_ref, half_ref, b1_ref, a1_ref, b2_ref, b3_ref, csem, rsem, ssem):
+    _, _, pos = place()
+    partner = peer_on(pos, "core", 1 - pos["core"])
+    peers = [partner] + [
+        peer_on(pos, d, lax.rem(pos[d] + r, RING)) for d in ("z", "x", "y") for r in range(1, RING)
+    ]
+    barrier = pltpu.get_barrier_semaphore()
+    for p in peers:
+        pl.semaphore_signal(barrier, inc=1, device_id=p, device_id_type=MESH)
+    pl.semaphore_wait(barrier, len(peers))
+
+    core = pos["core"]
+    mine = pl.multiple_of(core * HALF, PART)
+    other = pl.multiple_of((1 - core) * HALF, PART)
+    cs = [
+        send(
+            g_ref.at[pl.ds(pl.multiple_of(other + part * PART, PART), PART)],
+            half_ref.at[part],
+            csem.at[part],
+            csem.at[3 + part],
+            partner,
+        )
+        for part in range(3)
+    ]
+    c1 = []
+    for part, (d1, _, _) in enumerate(ORDERS):
+        cs[part].wait_recv()
+        half_ref[part] = half_ref[part] + g_ref[pl.ds(pl.multiple_of(mine + part * PART, PART), PART), :]
+        for r in (2, 1, 3):
+            to = lax.rem(pos[d1] + r, RING)
+            c1.append(
+                send(
+                    half_ref.at[part, pl.ds(pl.multiple_of(to * Q1, Q1), Q1)],
+                    b1_ref.at[part, r - 1],
+                    ssem.at[0, part, r - 1],
+                    rsem.at[0, part, r - 1],
+                    peer_on(pos, d1, to),
+                )
+            )
+    c2 = []
+    for part, (d1, d2, _) in enumerate(ORDERS):
+        for c in c1[3 * part : 3 * part + 3]:
+            c.wait_recv()
+        own = half_ref[part, pl.ds(pl.multiple_of(pos[d1] * Q1, Q1), Q1), :]
+        a1_ref[part] = own + b1_ref[part, 0] + (b1_ref[part, 1] + b1_ref[part, 2])
+        for r in (2, 1, 3):
+            to = lax.rem(pos[d2] + r, RING)
+            c2.append(
+                send(
+                    a1_ref.at[part, pl.ds(pl.multiple_of(to * Q2, Q2), Q2)],
+                    b2_ref.at[part, r - 1],
+                    ssem.at[1, part, r - 1],
+                    rsem.at[1, part, r - 1],
+                    peer_on(pos, d2, to),
+                )
+            )
+    c3 = []
+    for part, (d1, d2, d3) in enumerate(ORDERS):
+        for c in c2[3 * part : 3 * part + 3]:
+            c.wait_recv()
+        own = a1_ref[part, pl.ds(pl.multiple_of(pos[d2] * Q2, Q2), Q2), :]
+        b3_ref[part, pos[d3]] = own + b2_ref[part, 0] + (b2_ref[part, 1] + b2_ref[part, 2])
+        for r in (2, 1, 3):
+            to = lax.rem(pos[d3] + r, RING)
+            c3.append(
+                send(
+                    b3_ref.at[part, pos[d3]],
+                    b3_ref.at[part, pos[d3]],
+                    ssem.at[2, part, r - 1],
+                    rsem.at[2, part, r - 1],
+                    peer_on(pos, d3, to),
+                )
+            )
+    c4 = []
+    for part, (d1, d2, d3) in enumerate(ORDERS):
+        for c in c3[3 * part : 3 * part + 3]:
+            c.wait_recv()
+        start = pl.multiple_of(mine + part * PART + pos[d1] * Q1 + pos[d2] * Q2, Q2)
+        o_ref[pl.ds(start, Q2), :] = (b3_ref[part, 0] + b3_ref[part, 1]) + (b3_ref[part, 2] + b3_ref[part, 3])
+        here = o_ref.at[pl.ds(start, Q2)]
+        for r in (2, 1, 3):
+            to = lax.rem(pos[d2] + r, RING)
+            c4.append(send(here, here, ssem.at[3, part, r - 1], rsem.at[3, part, r - 1], peer_on(pos, d2, to)))
+    c5 = []
+    for part, (d1, d2, d3) in enumerate(ORDERS):
+        for c in c4[3 * part : 3 * part + 3]:
+            c.wait_recv()
+        here = o_ref.at[pl.ds(pl.multiple_of(mine + part * PART + pos[d1] * Q1, Q2), Q1)]
+        for r in (2, 1, 3):
+            to = lax.rem(pos[d1] + r, RING)
+            c5.append(send(here, here, ssem.at[4, part, r - 1], rsem.at[4, part, r - 1], peer_on(pos, d1, to)))
+    c6 = []
+    for part, (d1, d2, d3) in enumerate(ORDERS):
+        for c in c5[3 * part : 3 * part + 3]:
+            c.wait_recv()
+        here = o_ref.at[pl.ds(pl.multiple_of(mine + part * PART, PART), PART)]
+        c6.append(send(here, here, csem.at[6 + part], csem.at[9 + part], partner))
+    for c in c6:
+        c.wait_recv()
+    for c in cs + c1 + c2 + c3 + c4 + c5 + c6:
+        c.wait_send()
+
+
+def reduce_all(g):
+    return pl.pallas_call(
+        reduce_kernel,
+        out_shape=jax.ShapeDtypeStruct(g.shape, F32),
+        in_specs=[pl.BlockSpec(memory_space=pltpu.VMEM)],
+        out_specs=pl.BlockSpec(memory_space=pltpu.VMEM),
+        scratch_shapes=[
+            pltpu.VMEM((3, PART, BLK), F32),
+            pltpu.VMEM((3, RING - 1, Q1, BLK), F32),
+            pltpu.VMEM((3, Q1, BLK), F32),
+            pltpu.VMEM((3, RING - 1, Q2, BLK), F32),
+            pltpu.VMEM((3, RING, Q2, BLK), F32),
+            pltpu.SemaphoreType.DMA((12,)),
+            pltpu.SemaphoreType.DMA((5, 3, RING - 1)),
+            pltpu.SemaphoreType.DMA((5, 3, RING - 1)),
+        ],
+        compiler_params=pltpu.CompilerParams(collective_id=0, has_side_effects=True, vmem_limit_bytes=60 * 2**20),
+        name="reduce_all",
+    )(g)
+
+
+def solve_kernel(g_ref, c_ref, y_ref, a_ref, w_ref, m_ref, lh_ref, ll_ref, yh_ref, yl_ref, z_ref, csem, ysem):
+    n = c_ref.shape[0]
+    steps = n // BLK
+    loads = []
+    for k in range(steps):
+        rows = pl.ds(k * BLK, BLK)
+        loads.append(pltpu.make_async_copy(c_ref.at[rows], z_ref.at[rows], csem.at[k]))
+        loads[-1].start()
+    stores = []
+    for k in range(steps):
         lo, hi = k * BLK, (k + 1) * BLK
-        s = g_ref[lo:, lo:hi]
+        s = jnp.concatenate([g_ref[tile_row(i, k) : tile_row(i, k) + BLK, :] for i in range(k, steps)], axis=0)
         if k:
             s = s - dot3(lh_ref[lo:, :lo], ll_ref[lo:, :lo], lh_ref[lo:hi, :lo], ll_ref[lo:hi, :lo], NT)
         a_ref[...] = s[:BLK]
@@ -100,16 +271,22 @@
             lkh, lkl = split(dot3(sh, sl, mh, ml, NT))
             lh_ref[hi:, lo:hi] = lkh
             ll_ref[hi:, lo:hi] = lkl
-        z = c_ref[lo:hi, :]
+        loads[k].wait()
+        z = z_ref[lo:hi, :]
         if k:
             z = z - dot3(lh_ref[lo:hi, :lo], ll_ref[lo:hi, :lo], yh_ref[:lo, :], yl_ref[:lo, :], NN)
         zh, zl = split(z)
         y = dot3(mh, ml, zh, zl, NN)
-        y_ref[lo:hi, :] = y
+        z_ref[lo:hi, :] = y
+        rows = pl.ds(lo, BLK)
+        stores.append(pltpu.make_async_copy(z_ref.at[rows], y_ref.at[rows], ysem.at[k]))
+        stores[-1].start()
         if hi < n:
             yh, yl = split(y)
             yh_ref[lo:hi, :] = yh
             yl_ref[lo:hi, :] = yl
+    for c in stores:
+        c.wait()
 
 
 def solve(g, c):
@@ -117,37 +294,54 @@
     return pl.pallas_call(
         solve_kernel,
         out_shape=jax.ShapeDtypeStruct((n, w), F32),
-        in_specs=[pl.BlockSpec(memory_space=pltpu.VMEM)] * 2,
-        out_specs=pl.BlockSpec(memory_space=pltpu.VMEM),
+        in_specs=[pl.BlockSpec(memory_space=pltpu.VMEM), ANY],
+        out_specs=ANY,
         scratch_shapes=[pltpu.VMEM((BLK, BLK), F32)] * 3
         + [pltpu.VMEM((n, n), BF)] * 2
-        + [pltpu.VMEM((n, w), BF)] * 2,
+        + [pltpu.VMEM((n, w), BF)] * 2
+        + [pltpu.VMEM((n, w), F32), pltpu.SemaphoreType.DMA((n // BLK,)), pltpu.SemaphoreType.DMA((n // BLK,))],
         compiler_params=pltpu.CompilerParams(vmem_limit_bytes=60 * 2**20),
         name="solve",
     )(g, c)
 
 
-def gram_kernel(c_ref, g_ref, h_ref, l_ref):
+GB = 256
+
+
+def gram_kernel(c_ref, g_ref, x_ref, h_ref, l_ref, sem):
     n = c_ref.shape[0]
-    b = 256
-    for i in range(n // b):
-        h, l = split(c_ref[i * b : (i + 1) * b, :])
-        h_ref[i * b : (i + 1) * b, :] = h
-        l_ref[i * b : (i + 1) * b, :] = l
-        e = (i + 1) * b
-        g_ref[i * b : e, :e] = dot3(h, l, h_ref[:e, :], l_ref[:e, :], NT)
-        if e < n:
-            g_ref[i * b : e, e:] = jnp.zeros((b, n - e), F32)
+    loads = []
+    for i in range(n // GB):
+        rows = pl.ds(i * GB, GB)
+        loads.append(pltpu.make_async_copy(c_ref.at[rows], x_ref.at[rows], sem.at[i]))
+        loads[-1].start()
+    for i in range(n // GB):
+        lo, e = i * GB, (i + 1) * GB
+        loads[i].wait()
+        h, l = split(x_ref[lo:e, :])
+        h_ref[lo:e, :] = h
+        l_ref[lo:e, :] = l
+        g = dot3(h, l, h_ref[:e, :], l_ref[:e, :], NT)
+        for bi in range(lo // BLK, e // BLK):
+            for bj in range(bi + 1):
+                t = tile_row(bi, bj)
+                r = bi * BLK - lo
+                g_ref[t : t + BLK, :] = g[r : r + BLK, bj * BLK : (bj + 1) * BLK]
 
 
 def gram(c):
     n, w = c.shape
     return pl.pallas_call(
         gram_kernel,
-        out_shape=jax.ShapeDtypeStruct((n, n), F32),
-        in_specs=[pl.BlockSpec(memory_space=pltpu.VMEM)],
+        out_shape=jax.ShapeDtypeStruct((TILES * BLK, BLK), F32),
+        in_specs=[ANY],
         out_specs=pl.BlockSpec(memory_space=pltpu.VMEM),
-        scratch_shapes=[pltpu.VMEM((n, w), BF)] * 2,
+        scratch_shapes=[
+            pltpu.VMEM((n, w), F32),
+            pltpu.VMEM((n, w), BF),
+            pltpu.VMEM((n, w), BF),
+            pltpu.SemaphoreType.DMA((n // GB,)),
+        ],
         compiler_params=pltpu.CompilerParams(vmem_limit_bytes=60 * 2**20),
         name="gram",
     )(c)
@@ -156,45 +350,138 @@
 CH = 2048
 
 
-def scatter_kernel(idx_ref, r_ref, o_ref):
+def scatter_kernel(idx_ref, r_ref, o_ref, rows_ref, to_ref):
+    rows_ref[...] = r_ref[...].T
+
     def body(i, _):
         base = i * 16
         for u in range(16):
-            o_ref[pl.ds(idx_ref[base + u], 1), :] = r_ref[pl.ds(base + u, 1), :]
+            to_ref[pl.ds(idx_ref[base + u], 1), :] = rows_ref[pl.ds(base + u, 1), :]
         return 0
 
     lax.fori_loop(0, CH // 16, body, 0)
 
-
-def scatter_rows(idx, rows):
-    n, w = rows.shape
+    @pl.when(pl.program_id(0) == pl.num_programs(0) - 1)
+    def _():
+        for s in range(0, o_ref.shape[1], CH):
+            o_ref[:, s : s + CH] = to_ref[s : s + CH, :].T
+
+
+def scatter_columns(idx, r):
+    w, n = r.shape
     return pl.pallas_call(
         scatter_kernel,
         grid=(n // CH,),
-        out_shape=jax.ShapeDtypeStruct((n, w), F32),
+        out_shape=jax.ShapeDtypeStruct((w, n), F32),
         in_specs=[
             pl.BlockSpec((CH,), lambda i: (i,), memory_space=pltpu.SMEM),
-            pl.BlockSpec((CH, w), lambda i: (i, 0)),
+            pl.BlockSpec((w, CH), lambda i: (0, i)),
         ],
-        out_specs=pl.BlockSpec((n, w), lambda i: (0, 0)),
+        out_specs=pl.BlockSpec((w, n), lambda i: (0, 0)),
+        scratch_shapes=[pltpu.VMEM((CH, w), F32), pltpu.VMEM((n, w), F32)],
         compiler_params=pltpu.CompilerParams(vmem_limit_bytes=60 * 2**20),
         name="scatter",
-    )(idx, rows)
-
-
-from jax.sharding import PartitionSpec as P
-
-NB = 1024
-NGROUPS = 16
-
-
-def copy_for_each(x, axis):
-    copies = jnp.broadcast_to(x, (lax.axis_size(axis), *x.shape))
-    return lax.all_to_all(copies, axis, split_axis=0, concat_axis=0, tiled=True)
-
-
-def of_everyone(x, axis):
-    return copy_for_each(x, axis).sum(axis=0)
+    )(idx, r)
+
+
+def exchange(slots, index, peers, ssem, rsem):
+    here = slots.at[index]
+    copies = [send(here, here, ssem.at[r], rsem.at[r], p) for r, p in enumerate(peers)]
+    for c in copies:
+        c.wait_recv()
+    return copies
+
+
+def tail_kernel(b_ref, t_ref, grp_ref, o_ref, res_ref, tot_ref,
+                land_ref, want_ref, sq_ref, gr_ref, isem, tsem, osem, s2, r2, s3, r3):
+    band, coef, _ = place()
+    nband, bands, part = b_ref.shape
+    ncoef = sq_ref.shape[0]
+    bpeers = [(lax.rem(band + r, nband), coef) for r in range(1, nband)]
+    cpeers = [(band, lax.rem(coef + r, ncoef)) for r in range(1, ncoef)]
+    ins = []
+    for s in range(nband):
+        cols = pl.ds(s * part, part)
+        ins.append(
+            (
+                pltpu.make_async_copy(b_ref.at[s], land_ref.at[:, cols], isem.at[s]),
+                pltpu.make_async_copy(t_ref.at[:, cols], want_ref.at[:, cols], tsem.at[s]),
+            )
+        )
+        for c in ins[-1]:
+            c.start()
+    barrier = pltpu.get_barrier_semaphore()
+    for p in bpeers + cpeers:
+        pl.semaphore_signal(barrier, inc=1, device_id=p, device_id_type=MESH)
+    pl.semaphore_wait(barrier, nband + ncoef - 2)
+    acc = jnp.zeros((bands, BLK), F32)
+    outs = []
+    for s in range(nband):
+        for c in ins[s]:
+            c.wait()
+        cols = pl.ds(s * part, part)
+        outs.append(pltpu.make_async_copy(land_ref.at[:, cols], o_ref.at[:, cols], osem.at[s]))
+        outs[-1].start()
+        d = land_ref[:, s * part : (s + 1) * part] - want_ref[:, s * part : (s + 1) * part]
+        d = d * d
+        for q in range(0, part, BLK):
+            acc = acc + d[:, q : q + BLK]
+    row = lax.broadcasted_iota(jnp.int32, (bands, BLK), 0)
+    lane = lax.broadcasted_iota(jnp.int32, (bands, BLK), 1)
+    total = jnp.sum(acc, axis=1, keepdims=True)
+    line = jnp.sum(jnp.where(row == lane, total, 0.0), axis=0, keepdims=True)
+    sq_ref[coef] = jnp.broadcast_to(line, (8, BLK))
+    c2 = exchange(sq_ref, coef, cpeers, s2, r2)
+    tot = sq_ref[0]
+    for q in range(1, ncoef):
+        tot = tot + sq_ref[q]
+    res = jnp.sqrt(tot + 1e-06)
+    res_ref[...] = res
+    g16 = lax.broadcasted_iota(jnp.int32, (NGROUPS, BLK), 0)
+    gr_ref[band] = jnp.where(g16 == grp_ref[0:1, :], res[0:1, :], 0.0)
+    c3 = exchange(gr_ref, band, bpeers, s3, r3)
+    g = gr_ref[0]
+    for q in range(1, nband):
+        g = g + gr_ref[q]
+    tot_ref[...] = jnp.broadcast_to(jnp.sum(g, axis=1, keepdims=True), (NGROUPS, BLK)) * (NGROUPS / NB)
+    for c in outs:
+        c.wait()
+    for c in c2 + c3:
+        c.wait_send()
+
+
+def tail(b, t, grp):
+    vm = pl.BlockSpec(memory_space=pltpu.VMEM)
+    bands, width = t.shape
+    nband = b.shape[0]
+    ncoef = lax.axis_size("coef")
+    return pl.pallas_call(
+        tail_kernel,
+        out_shape=(
+            jax.ShapeDtypeStruct((bands, width), F32),
+            jax.ShapeDtypeStruct((8, BLK), F32),
+            jax.ShapeDtypeStruct((NGROUPS, BLK), F32),
+        ),
+        in_specs=[ANY, ANY, vm],
+        out_specs=(ANY, vm, vm),
+        scratch_shapes=[
+            pltpu.VMEM((bands, width), F32),
+            pltpu.VMEM((bands, width), F32),
+            pltpu.VMEM((ncoef, 8, BLK), F32),
+            pltpu.VMEM((nband, NGROUPS, BLK), F32),
+            pltpu.SemaphoreType.DMA((nband,)),
+            pltpu.SemaphoreType.DMA((nband,)),
+            pltpu.SemaphoreType.DMA((nband,)),
+            pltpu.SemaphoreType.DMA((ncoef - 1,)),
+            pltpu.SemaphoreType.DMA((ncoef - 1,)),
+            pltpu.SemaphoreType.DMA((nband - 1,)),
+            pltpu.SemaphoreType.DMA((nband - 1,)),
+        ],
+        compiler_params=pltpu.CompilerParams(
+            collective_id=1, has_side_effects=True, vmem_limit_bytes=60 * 2**20
+        ),
+        name="tail",
+    )(b, t, grp)
 
 
 def local(coeffs, ref_block, index_map, band_group):
@@ -204,21 +491,13 @@
     blocks = coeffs.reshape(bands, parts, part).transpose(1, 0, 2)
     columns = lax.all_to_all(blocks, "band", split_axis=0, concat_axis=0, tiled=True)
     columns = columns.reshape(parts * bands, part)
-    moved = scatter_rows(index_map, ref_block.T).T
-    margin = lax.psum(gram(columns), ("band", "coef"))
+    moved = scatter_columns(index_map, ref_block)
+    margin = reduce_all(gram(columns))
     ortho_cols = solve(margin, columns).reshape(parts, bands, part)
     back = lax.all_to_all(ortho_cols, "band", split_axis=0, concat_axis=0, tiled=True)
-    ortho = back.transpose(1, 0, 2).reshape(bands, width)
-    squares = jnp.sum((ortho - moved) ** 2, axis=1)
-    group_range = jnp.arange(NGROUPS, dtype=jnp.int32)
-    totals = of_everyone(squares, "coef")
-    band_residual = jnp.sqrt(totals + 1e-06)
-    onehot = (band_group[:, None] == group_range[None, :]).astype(F32)
-    terms = jnp.dot(
-        band_residual, onehot, precision=lax.Precision.HIGHEST, preferred_element_type=F32
-    )
-    group_residual = of_everyone(terms, "band") * (NGROUPS / NB)
-    return (ortho, band_residual, group_residual)
+    groups = jnp.broadcast_to(jnp.pad(band_group, (0, BLK - bands), constant_values=-1), (8, BLK))
+    ortho, res, tot = tail(back, moved, groups)
+    return (ortho, res[0, :bands], tot[:, 0])
 
 
 def solution(mesh):

time: 559 us -> 404 us (0.72)
  waiting for transfers between devices: 223 us -> 77.3 us
  Pallas kernels: 143 us -> 203 us
  local copies, waits for them, and re-layouts: 41.7 us -> 14.5 us
  between operations: 14.1 us -> 0.7 us
  other arithmetic: 12.5 us -> 0 us
  blocking collectives: 115 us -> 103 us
    psum x1 -> x0, waiting for transfers between devices: 153 us -> none  [local(): margin = lax.psum(gram(columns), ('band', 'coef'))]
    pallas_call x2 -> x4, Pallas kernels: 56.6 us -> 120 us  [the longest x1 50 us: scatter_columns(): pl.pallas_call(scatter_kernel, grid=(n // CH,), out_shape=jax.ShapeDtypeS...]
    unnamed x6 -> x3, local copies, waits for them, and re-layouts: 24.9 us -> 7.39 us
    transpose x1 -> x0, local copies, waits for them, and re-layouts: 12.2 us -> none  [local(): ortho = back.transpose(1, 0, 2).reshape(bands, width)]
    reduce_sum x3 -> x0, other arithmetic: 12 us -> none  [the longest x1 12 us: local(): squares = jnp.sum((ortho - moved) ** 2, axis=1)]
    all_to_all x1 -> x0, blocking collectives: 11.9 us -> none  [copy_for_each(): return lax.all_to_all(copies, axis, split_axis=0, concat_axis=0, tiled=True)]
    all_to_all x1, waiting for transfers between devices: 69 us -> 77.3 us  [local(): lax.all_to_all(ortho_cols, 'band', split_axis=0, concat_axis=0, tiled=True)]
  transfers between devices with their start and end apart: 3 -> 1, of which waited for: 2 -> 1; matrix products, arithmetic and copies ran while one was open for 4% -> 0% of each run, Pallas kernels for 8% -> 12%
where the time goes in v2:
time: 404 us; the launch traced here: 403 us
  Pallas kernels  203 us (50%)
  blocking collectives  103 us (25%)
  waiting for transfers between devices  77.3 us (19%)
  local copies, waits for them, and re-layouts  14.5 us (4%)
  starting transfers between devices  4.74 us (1%)
    all_to_all x1, blocking collectives, local(): lax.all_to_all(blocks, 'band', split_axis=0, concat_axis=0, tiled=True)  103 us
    pallas_call x1, Pallas kernels, solve(): pl.pallas_call(solve_kernel, out_shape=jax.ShapeDtypeStruct((n, w), F32),...  83 us
    all_to_all x1, waiting for transfers between devices, local(): lax.all_to_all(ortho_cols, 'band', split_axis=0, concat_axis=0, tiled=True)  77.3 us
    pallas_call x1, Pallas kernels, scatter_columns(): pl.pallas_call(scatter_kernel, grid=(n // CH,), out_shape=jax.ShapeDtypeS...  50 us
    pallas_call x1, Pallas kernels, reduce_all(): pl.pallas_call(reduce_kernel, out_shape=jax.ShapeDtypeStruct(g.shape, F32...  34.9 us
    pallas_call x1, Pallas kernels, gram(): pl.pallas_call(gram_kernel, out_shape=jax.ShapeDtypeStruct((TILES * BLK,...  18.4 us
    pallas_call x1, Pallas kernels, tail(): pl.pallas_call(tail_kernel, out_shape=(jax.ShapeDtypeStruct((bands, width...  16.9 us
  transfers between devices with their start and end apart: 1, of which 1 were waited for; matrix products, arithmetic and copies ran while one was open for 0% of the time, Pallas kernels for 12%

profile of v2, /device:TPU:1, one launch (start us, length us, event | category | flops | bytes accessed | tf_op | source)
XLA Modules:
  0.0 403.4 jit_solution(15983441567770070845)
XLA Ops:
  0.6 4.0 copy.11
  4.6 103.0 %all_to_all.10 = f32[16,64,2048]{2,1,0:T(8,128)} all-to-all(f32[16,64,2048]{2,1,0:T(8,128)S(1)} %bitcast.14), channel_id=1, replica_groups=mesh['band'=16,'coef'=8] {'band'}, dimensions={0} | all-to-all | bytes 16777216 | tf_op jit(solution)/shard_map/all_to_all | solution.py:492
  107.6 18.4 %gram.1.g_ref = f32[4608,128]{1,0:T(8,128)} custom-call(f32[1024,2048]{1,0:T(8,128)} %bitcast.11), custom_call_target="tpu_custom_call" | custom-call | tf_op jit(solution)/shard_map/gram/pallas_call | solution.py:334
  126.0 34.9 %reduce_all.1.g_ref = f32[4608,128]{1,0:T(8,128)} custom-call(f32[4608,128]{1,0:T(8,128)} %gram.1.g_ref), custom_call_target="tpu_custom_call" | custom-call | tf_op jit(solution)/shard_map/reduce_all/pallas_call | solution.py:232
  160.9 83.0 %solve.1 = f32[1024,2048]{1,0:T(8,128)} custom-call(f32[4608,128]{1,0:T(8,128)} %reduce_all.1.g_ref, f32[1024,2048]{1,0:T(8,128)} %bitcast.12), custom_call_target="tpu_custom_call" | custom-call | tf_op jit(solution)/shard_map/solve/pallas_call | solution.py:294
  244.0 0.0 copy-start
  244.0 4.7 %all-to-all-start.1 = ((f32[16,64,2048]{2,1,0:T(8,128)}), f32[16,64,2048]{2,1,0:T(8,128)}, u32[]{:S(2)}, u32[]{:S(2)}) async-start(f32[16,64,2048]{2,1,0:T(8,128)} %bitcast.13), calls=%async_computation.1 | async-start | bytes 16777216 | tf_op jit(solution)/shard_map/all_to_all | solution.py:497
  248.7 0.0 copy-done
  248.7 50.0 %scatter.1.t_ref = f32[64,32768]{1,0:T(8,128)} custom-call(s32[32768]{0:T(1024)} %idx_ref.1, f32[64,32768]{1,0:T(8,128)} %r_ref.1), custom_call_target="tpu_custom_call" | custom-call | tf_op jit(solution)/shard_map/scatter/pallas_call | solution.py:372
  298.8 77.3 %all-to-all-done.1.b_ref = f32[16,64,2048]{2,1,0:T(8,128)} async-done(((f32[16,64,2048]{2,1,0:T(8,128)}), f32[16,64,2048]{2,1,0:T(8,128)}, u32[]{:S(2)}, u32[]{:S(2)}) %all-to-all-start.1) | async-done | bytes 8388640 | tf_op jit(solution)/shard_map/all_to_all | solution.py:497
  376.1 0.6 broadcast_in_dim.3.grp_ref
  376.7 16.9 %tail.1 = (f32[64,32768]{1,0:T(8,128)}, f32[8,128]{1,0:T(8,128)}, f32[16,128]{1,0:T(8,128)}) custom-call(f32[16,64,2048]{2,1,0:T(8,128)} %all-to-all-done.1.b_ref, f32[64,32768]{1,0:T(8,128)} %scatter.1.t_ref, s32[8,128]{1,0:T(8,128)} %broadcast_in_dim.3.grp_ref), custom_call_target="tpu_custom_call" | custom-call | tf_op jit(solution)/shard_map/tail/pallas_call | solution.py:458
  393.5 1.2 slice_bitcast_fusion
  394.7 1.3 slice_reduce_fusion
  396.1 7.4 %copy.13 = f32[64,32768]{1,0:T(8,128)} copy(f32[64,32768]{1,0:T(8,128)} %get-tuple-element.12) | data formatting | bytes 16777216
  (1 shorter events, 0.0 us)
Async XLA Ops:
  244.0 4.8 %copy-start = (s32[64]{0:T(128)S(1)}, s32[64]{0:T(128)}, u32[]{:S(2)}) copy-start(s32[64]{0:T(128)} %param.7) | copy-start | bytes 772
  244.0 132.1 %all-to-all-start.1 = ((f32[16,64,2048]{2,1,0:T(8,128)}), f32[16,64,2048]{2,1,0:T(8,128)}, u32[]{:S(2)}, u32[]{:S(2)}) async-start(f32[16,64,2048]{2,1,0:T(8,128)} %bitcast.13), calls=%async_computation.1 | async-start | bytes 16777216 | tf_op jit(solution)/shard_map/all_to_all | solution.py:497

commit v3 on v2

--- a/solution.py
+++ b/solution.py
@@ -91,7 +91,7 @@
 NGROUPS = 16
 NBLK = NB // BLK
 TILES = NBLK * (NBLK + 1) // 2
-ANY = pl.BlockSpec(memory_space=pl.ANY)
+ANY = pl.BlockSpec(memory_space=pltpu.HBM)
 
 
 def tile_row(i, j):
@@ -347,41 +347,276 @@
     )(c)
 
 
+HR = 32
+
+
+def ring_kernel(to_rows, side, c_ref, o_ref, src_ref, land_ref, b1_ref, r1_ref, r2_ref,
+                lsem, osem, s1, v1, sr1, vr1, sf1, s2, v2, sr2, vr2, sf2, qsem):
+    band, coef, pos = place()
+    part = 2048
+    bands = 64
+    dims = (("z", "x"), ("x", "z"))
+
+    def who(h, a, b):
+        d1, d2 = dims[h]
+        p = dict(pos)
+        p[d1] = lax.rem(pos[d1] + a + RING, RING)
+        p[d2] = lax.rem(pos[d2] + b + RING, RING)
+        return p["z"] * 4 + p["x"]
+
+    def wide(h, b):
+        return (pl.ds(h * HR, HR), pl.ds(pl.multiple_of(b * part, part), part))
+
+    def tall(h, b):
+        return (pl.ds(pl.multiple_of(b * bands + h * HR, HR), HR), slice(None))
+
+    far = tall if to_rows else wide
+
+    def cell(h, b):
+        return (b, pl.ds(h * HR, HR))
+
+    loads = {}
+    for a in range(RING):
+        for b in range(RING):
+            d = who(0, a, b)
+            at = (slice(None), pl.ds(pl.multiple_of(d * part, part), part)) if to_rows else (
+                pl.ds(pl.multiple_of(d * bands, bands), bands), slice(None))
+            loads[a, b] = pltpu.make_async_copy(c_ref.at[at], src_ref.at[d], lsem.at[a, b])
+    order = [(2, 1), (1, 2), (2, 3), (3, 2), (2, 2), (2, 0), (0, 2)]
+    order += [k for k in loads if k not in order and k != (0, 0)] + [(0, 0)]
+    for k in order:
+        loads[k].start()
+    barrier = pltpu.get_barrier_semaphore()
+    near_by = [(h, s) for h in range(2) for s in (1, -1)]
+    for h, s in near_by:
+        pl.semaphore_signal(barrier, inc=1, device_id=(who(h, s, 0), coef), device_id_type=MESH)
+    pl.semaphore_wait(barrier, 4)
+
+    ready = set()
+
+    def src(h, a, b):
+        k = (a, b) if h == 0 else (b, a)
+        if k not in ready:
+            loads[k].wait()
+            ready.add(k)
+        return src_ref.at[cell(h, who(h, a, b))]
+
+    sent = []
+
+    def go(*args):
+        sent.append(send(*args))
+        return sent[-1]
+
+    SIGN = (1, -1)
+    VIA1 = ((2, 1), (3, 0))
+    VIA2 = ((0, 1), (3, 2))
+    rel1 = {}
+    for i in range(2):
+        for h in range(2):
+            for g in range(2):
+                q = VIA1[g][i]
+                rel1[h, g, i] = go(src(h, 2, q), r1_ref.at[h, g, i], sr1.at[h, g, i], vr1.at[h, g, i],
+                                   (who(h, SIGN[g], 0), coef))
+    dir1 = {}
+    for q in (2, 1, 3, 0):
+        for h in range(2):
+            for g in range(2):
+                r = 1 if g == 0 else 3
+                dir1[h, r, q] = go(src(h, r, q), b1_ref.at[h, r - 1, q], s1.at[h, r - 1, q], v1.at[h, r - 1, q],
+                                   (who(h, SIGN[g], 0), coef))
+    side(0)
+    for i in range(2):
+        for h in range(2):
+            for g in range(2):
+                q = VIA1[g][i]
+                rel1[h, g, i].wait_recv()
+                dir1[h, 2, q] = go(r1_ref.at[h, g, i], b1_ref.at[h, 1, q], sf1.at[h, g, i], v1.at[h, 1, q],
+                                   (who(h, SIGN[g], 0), coef))
+    rel2, fin, outs = {}, {}, []
+
+    def second(h, r, q):
+        block = src(h, 0, q) if r == 0 else b1_ref.at[h, r - 1, q]
+        if q == 0:
+            at = far(h, who(h, -r, 0))
+            outs.append(pltpu.make_async_copy(block, o_ref.at[at], qsem.at[h, r]))
+            outs[-1].start()
+        elif q == 2:
+            g = 0 if r in VIA2[0] else 1
+            i = VIA2[g].index(r)
+            rel2[h, g, i] = go(block, r2_ref.at[h, g, i], sr2.at[h, g, i], vr2.at[h, g, i],
+                               (who(h, 0, SIGN[g]), coef))
+        else:
+            at = land_ref.at[cell(h, who(h, -r, 0))]
+            fin[h, r, q] = go(block, at, s2.at[h, r, q - 1], v2.at[h, r, q - 1],
+                              (who(h, 0, 1 if q == 1 else -1), coef))
+
+    for q in (2, 1, 3, 0):
+        for h in range(2):
+            second(h, 0, q)
+    side(1)
+    for q in (2, 1, 3, 0):
+        for r in (1, 3):
+            for h in range(2):
+                dir1[h, r, q].wait_recv()
+                second(h, r, q)
+    for q in (2, 1, 3, 0):
+        for h in range(2):
+            dir1[h, 2, q].wait_recv()
+            second(h, 2, q)
+    side(2)
+    for i in range(2):
+        for h in range(2):
+            for g in range(2):
+                r = VIA2[g][i]
+                rel2[h, g, i].wait_recv()
+                at = land_ref.at[cell(h, who(h, -r, -SIGN[g]))]
+                fin[h, r, 2] = go(r2_ref.at[h, g, i], at, sf2.at[h, g, i], v2.at[h, r, 1],
+                                  (who(h, 0, SIGN[g]), coef))
+    for r in (0, 1, 3, 2):
+        for q in (1, 3, 2):
+            for h in range(2):
+                fin[h, r, q].wait_recv()
+                b = who(h, -r, -q)
+                outs.append(
+                    pltpu.make_async_copy(land_ref.at[cell(h, b)], o_ref.at[far(h, b)], osem.at[h, r, q - 1])
+                )
+                outs[-1].start()
+    for c in outs:
+        c.wait()
+    for c in sent:
+        c.wait_send()
+
+
+RING_SCRATCH = [
+    pltpu.VMEM((16, 64, 2048), F32),
+    pltpu.VMEM((16, 64, 2048), F32),
+    pltpu.VMEM((2, 3, 4, HR, 2048), F32),
+    pltpu.VMEM((2, 2, 2, HR, 2048), F32),
+    pltpu.VMEM((2, 2, 2, HR, 2048), F32),
+] + [
+    pltpu.SemaphoreType.DMA(s)
+    for s in (
+        (4, 4), (2, 4, 3), (2, 3, 4), (2, 3, 4), (2, 2, 2), (2, 2, 2), (2, 2, 2),
+        (2, 4, 3), (2, 4, 3), (2, 2, 2), (2, 2, 2), (2, 2, 2), (2, 4),
+    )
+]
+
+
+def collect_kernel(c_ref, o_ref, *scratch):
+    ring_kernel(False, lambda n: None, c_ref, o_ref, *scratch)
+
+
+def collect(c):
+    n, w = c.shape
+    return pl.pallas_call(
+        collect_kernel,
+        out_shape=jax.ShapeDtypeStruct((n // 16, w * 16), F32),
+        in_specs=[ANY],
+        out_specs=ANY,
+        scratch_shapes=RING_SCRATCH,
+        compiler_params=pltpu.CompilerParams(
+            collective_id=3, has_side_effects=True, vmem_limit_bytes=60 * 2**20
+        ),
+        name="collect",
+    )(c)
+
+
 CH = 2048
-
-
-def scatter_kernel(idx_ref, r_ref, o_ref, rows_ref, to_ref):
-    rows_ref[...] = r_ref[...].T
-
-    def body(i, _):
-        base = i * 16
-        for u in range(16):
-            to_ref[pl.ds(idx_ref[base + u], 1), :] = rows_ref[pl.ds(base + u, 1), :]
-        return 0
-
-    lax.fori_loop(0, CH // 16, body, 0)
-
-    @pl.when(pl.program_id(0) == pl.num_programs(0) - 1)
-    def _():
-        for s in range(0, o_ref.shape[1], CH):
-            o_ref[:, s : s + CH] = to_ref[s : s + CH, :].T
-
-
-def scatter_columns(idx, r):
-    w, n = r.shape
+STOPS = (0, 12, 16)
+
+
+def spread_kernel(inv_ref, c_ref, q_ref, o_ref, t_ref, q_all, rows_ref, got_ref, want_ref, isem, tsem, *scratch):
+    bands, width = q_ref.shape
+    n = width // CH
+    loads = []
+    for s in range(n):
+        cols = pl.ds(s * CH, CH)
+        loads.append(pltpu.make_async_copy(q_ref.at[:, cols], q_all.at[:, cols], isem.at[s]))
+    stores = [
+        pltpu.make_async_copy(want_ref.at[s % 2], t_ref.at[:, pl.ds(s * CH, CH)], tsem.at[s]) for s in range(n)
+    ]
+
+    def gather(s):
+        def body(i, _):
+            at = i * 16
+            for u in range(16):
+                got_ref[pl.ds(at + u, 1), :] = rows_ref[pl.ds(inv_ref[s * CH + at + u], 1), :]
+            return 0
+
+        lax.fori_loop(0, CH // 16, body, 0)
+        if s >= 2:
+            stores[s - 2].wait()
+        want_ref[s % 2] = got_ref[...].T
+        stores[s].start()
+
+    def side(stage):
+        if stage == 0:
+            for c in loads:
+                c.start()
+            for s, c in enumerate(loads):
+                c.wait()
+                rows_ref[s * CH : (s + 1) * CH, :] = q_all[:, s * CH : (s + 1) * CH].T
+        else:
+            for s in range(STOPS[stage - 1], STOPS[stage]):
+                gather(s)
+
+    ring_kernel(True, side, c_ref, o_ref, *scratch)
+    for c in stores[-2:]:
+        c.wait()
+
+
+def spread(inv, c, q):
+    a, b = c.shape
+    n = b // CH
     return pl.pallas_call(
-        scatter_kernel,
-        grid=(n // CH,),
-        out_shape=jax.ShapeDtypeStruct((w, n), F32),
-        in_specs=[
-            pl.BlockSpec((CH,), lambda i: (i,), memory_space=pltpu.SMEM),
-            pl.BlockSpec((w, CH), lambda i: (0, i)),
+        spread_kernel,
+        out_shape=(jax.ShapeDtypeStruct((a * 16, b // 16), F32), jax.ShapeDtypeStruct(q.shape, F32)),
+        in_specs=[pl.BlockSpec(memory_space=pltpu.SMEM), ANY, ANY],
+        out_specs=(ANY, ANY),
+        scratch_shapes=[
+            pltpu.VMEM((a, b), F32),
+            pltpu.VMEM((b, a), F32),
+            pltpu.VMEM((CH, a), F32),
+            pltpu.VMEM((2, a, CH), F32),
+            pltpu.SemaphoreType.DMA((n,)),
+            pltpu.SemaphoreType.DMA((n,)),
+            *RING_SCRATCH,
         ],
-        out_specs=pl.BlockSpec((w, n), lambda i: (0, 0)),
-        scratch_shapes=[pltpu.VMEM((CH, w), F32), pltpu.VMEM((n, w), F32)],
+        compiler_params=pltpu.CompilerParams(
+            collective_id=2, has_side_effects=True, vmem_limit_bytes=60 * 2**20
+        ),
+        name="spread",
+    )(inv, c, q)
+
+
+def invert_kernel(idx_ref, inv_ref):
+    n, w = idx_ref.shape
+    his = n * w // BLK
+    acc = jnp.zeros((his, 2 * BLK), F32)
+    for c in range(n):
+        idx = idx_ref[c : c + 1, :]
+        at = c * w + lax.broadcasted_iota(jnp.int32, (1, w), 1)
+        one = lax.broadcasted_iota(jnp.int32, (his, w), 0) == (idx >> 7)
+        low = lax.broadcasted_iota(jnp.int32, (BLK, w), 0) == (idx & 127)
+        hot = jnp.where(one, 1.0, 0.0).astype(BF)
+        top = jnp.where(low, (at >> 7).astype(F32), 0.0).astype(BF)
+        bot = jnp.where(low, (at & 127).astype(F32), 0.0).astype(BF)
+        both = jnp.concatenate([top, bot], axis=0)
+        acc = acc + lax.dot_general(hot, both, (NT, ((), ())), preferred_element_type=F32)
+    inv_ref[...] = acc[:, :BLK].astype(jnp.int32) * BLK + acc[:, BLK:].astype(jnp.int32)
+
+
+def invert(idx):
+    n = idx.shape[0]
+    out = pl.pallas_call(
+        invert_kernel,
+        out_shape=jax.ShapeDtypeStruct((n // BLK, BLK), jnp.int32),
+        in_specs=[pl.BlockSpec(memory_space=pltpu.VMEM)],
+        out_specs=pl.BlockSpec(memory_space=pltpu.VMEM),
         compiler_params=pltpu.CompilerParams(vmem_limit_bytes=60 * 2**20),
-        name="scatter",
-    )(idx, r)
+        name="invert",
+    )(idx.reshape(16, n // 16))
+    return out.reshape(n)
 
 
 def exchange(slots, index, peers, ssem, rsem):
@@ -392,10 +627,12 @@
     return copies
 
 
-def tail_kernel(b_ref, t_ref, grp_ref, o_ref, res_ref, tot_ref,
-                land_ref, want_ref, sq_ref, gr_ref, isem, tsem, osem, s2, r2, s3, r3):
+def tail_kernel(b_ref, t_ref, grp_ref, res_ref, tot_ref,
+                land_ref, want_ref, sq_ref, gr_ref, isem, tsem, s2, r2, s3, r3):
     band, coef, _ = place()
-    nband, bands, part = b_ref.shape
+    bands, width = b_ref.shape
+    nband = gr_ref.shape[0]
+    part = width // nband
     ncoef = sq_ref.shape[0]
     bpeers = [(lax.rem(band + r, nband), coef) for r in range(1, nband)]
     cpeers = [(band, lax.rem(coef + r, ncoef)) for r in range(1, ncoef)]
@@ -404,7 +641,7 @@
         cols = pl.ds(s * part, part)
         ins.append(
             (
-                pltpu.make_async_copy(b_ref.at[s], land_ref.at[:, cols], isem.at[s]),
+                pltpu.make_async_copy(b_ref.at[:, cols], land_ref.at[:, cols], isem.at[s]),
                 pltpu.make_async_copy(t_ref.at[:, cols], want_ref.at[:, cols], tsem.at[s]),
             )
         )
@@ -415,13 +652,9 @@
         pl.semaphore_signal(barrier, inc=1, device_id=p, device_id_type=MESH)
     pl.semaphore_wait(barrier, nband + ncoef - 2)
     acc = jnp.zeros((bands, BLK), F32)
-    outs = []
     for s in range(nband):
         for c in ins[s]:
             c.wait()
-        cols = pl.ds(s * part, part)
-        outs.append(pltpu.make_async_copy(land_ref.at[:, cols], o_ref.at[:, cols], osem.at[s]))
-        outs[-1].start()
         d = land_ref[:, s * part : (s + 1) * part] - want_ref[:, s * part : (s + 1) * part]
         d = d * d
         for q in range(0, part, BLK):
@@ -444,8 +677,6 @@
     for q in range(1, nband):
         g = g + gr_ref[q]
     tot_ref[...] = jnp.broadcast_to(jnp.sum(g, axis=1, keepdims=True), (NGROUPS, BLK)) * (NGROUPS / NB)
-    for c in outs:
-        c.wait()
     for c in c2 + c3:
         c.wait_send()
 
@@ -453,23 +684,21 @@
 def tail(b, t, grp):
     vm = pl.BlockSpec(memory_space=pltpu.VMEM)
     bands, width = t.shape
-    nband = b.shape[0]
+    nband = lax.axis_size("band")
     ncoef = lax.axis_size("coef")
     return pl.pallas_call(
         tail_kernel,
         out_shape=(
-            jax.ShapeDtypeStruct((bands, width), F32),
             jax.ShapeDtypeStruct((8, BLK), F32),
             jax.ShapeDtypeStruct((NGROUPS, BLK), F32),
         ),
         in_specs=[ANY, ANY, vm],
-        out_specs=(ANY, vm, vm),
+        out_specs=(vm, vm),
         scratch_shapes=[
             pltpu.VMEM((bands, width), F32),
             pltpu.VMEM((bands, width), F32),
             pltpu.VMEM((ncoef, 8, BLK), F32),
             pltpu.VMEM((nband, NGROUPS, BLK), F32),
-            pltpu.SemaphoreType.DMA((nband,)),
             pltpu.SemaphoreType.DMA((nband,)),
             pltpu.SemaphoreType.DMA((nband,)),
             pltpu.SemaphoreType.DMA((ncoef - 1,)),
@@ -485,18 +714,12 @@
 
 
 def local(coeffs, ref_block, index_map, band_group):
-    bands, width = coeffs.shape
-    parts = lax.axis_size("band")
-    part = width // parts
-    blocks = coeffs.reshape(bands, parts, part).transpose(1, 0, 2)
-    columns = lax.all_to_all(blocks, "band", split_axis=0, concat_axis=0, tiled=True)
-    columns = columns.reshape(parts * bands, part)
-    moved = scatter_columns(index_map, ref_block)
+    bands, _ = coeffs.shape
+    columns, moved = spread(invert(index_map), coeffs, ref_block)
     margin = reduce_all(gram(columns))
-    ortho_cols = solve(margin, columns).reshape(parts, bands, part)
-    back = lax.all_to_all(ortho_cols, "band", split_axis=0, concat_axis=0, tiled=True)
+    ortho = collect(solve(margin, columns))
     groups = jnp.broadcast_to(jnp.pad(band_group, (0, BLK - bands), constant_values=-1), (8, BLK))
-    ortho, res, tot = tail(back, moved, groups)
+    res, tot = tail(ortho, moved, groups)
     return (ortho, res[0, :bands], tot[:, 0])
 
 

time: 404 us -> 380 us (0.941); the launches traced: 403 us -> 374 us
  Pallas kernels: 203 us -> 361 us
  blocking collectives: 103 us -> 0 us
  waiting for transfers between devices: 77.3 us -> 0 us
  starting transfers between devices: 4.74 us -> 0 us
    pallas_call x2 -> x4, Pallas kernels: 66.9 us -> 224 us  [the longest x1 104 us: spread(): pl.pallas_call(spread_kernel, out_shape=(jax.ShapeDtypeStruct((a * 16, b...]
    all_to_all x1 -> x0, blocking collectives: 103 us -> none  [local(): lax.all_to_all(blocks, 'band', split_axis=0, concat_axis=0, tiled=True)]
    all_to_all x1 -> x0, waiting for transfers between devices: 77.3 us -> none  [local(): lax.all_to_all(ortho_cols, 'band', split_axis=0, concat_axis=0, tiled=True)]
    all_to_all x1 -> x0, starting transfers between devices: 4.74 us -> none  [local(): lax.all_to_all(ortho_cols, 'band', split_axis=0, concat_axis=0, tiled=True)]
  transfers between devices with their start and end apart: 1 -> 0, of which waited for: 1 -> 0; matrix products, arithmetic and copies ran while one was open for 0% -> 0% of each run, Pallas kernels for 12% -> 0%
where the time goes in v3:
time: 380 us; the launch traced here: 374 us
  Pallas kernels  361 us (95%)
  local copies, waits for them, and re-layouts  12.1 us (3%)
    pallas_call x1, Pallas kernels, spread(): pl.pallas_call(spread_kernel, out_shape=(jax.ShapeDtypeStruct((a * 16, b...  104 us
    pallas_call x1, Pallas kernels, collect(): pl.pallas_call(collect_kernel, out_shape=jax.ShapeDtypeStruct((n // 16, w...  97.7 us
    pallas_call x1, Pallas kernels, solve(): pl.pallas_call(solve_kernel, out_shape=jax.ShapeDtypeStruct((n, w), F32),...  83.1 us
    pallas_call x1, Pallas kernels, reduce_all(): pl.pallas_call(reduce_kernel, out_shape=jax.ShapeDtypeStruct(g.shape, F32...  34.9 us
    pallas_call x1, Pallas kernels, gram(): pl.pallas_call(gram_kernel, out_shape=jax.ShapeDtypeStruct((TILES * BLK,...  18.4 us
    pallas_call x1, Pallas kernels, tail(): pl.pallas_call(tail_kernel, out_shape=(jax.ShapeDtypeStruct((8, BLK), F32...  15.8 us

profile of v3, /device:TPU:1, one launch (start us, length us, event | category | flops | bytes accessed | tf_op | source)
XLA Modules:
  0.0 373.8 jit_solution(15257425937971352334)
XLA Ops:
  0.6 1.6 reshape.12.idx_ref
  2.2 6.9 %invert.1 = s32[256,128]{1,0:T(8,128)} custom-call(s32[16,2048]{1,0:T(8,128)} %reshape.12.idx_ref), custom_call_target="tpu_custom_call" | custom-call | tf_op jit(solution)/shard_map/invert/pallas_call | solution.py:611
  9.1 103.8 %spread.1 = (f32[1024,2048]{1,0:T(8,128)}, f32[64,32768]{1,0:T(8,128)}) custom-call(s32[32768]{0:T(1024)} %bitcast.3, f32[64,32768]{1,0:T(8,128)} %c_ref.1, f32[64,32768]{1,0:T(8,128)} %q_ref.1), custom_call_target="tpu_custom_call" | custom-call | tf_op jit(solution)/shard_map/spread/pallas_call | solution.py:571
  113.0 18.4 %gram.1.g_ref = f32[4608,128]{1,0:T(8,128)} custom-call(f32[1024,2048]{1,0:T(8,128)} %get-tuple-element.7.c_ref), custom_call_target="tpu_custom_call" | custom-call | tf_op jit(solution)/shard_map/gram/pallas_call | solution.py:334
  131.4 34.9 %reduce_all.1.g_ref = f32[4608,128]{1,0:T(8,128)} custom-call(f32[4608,128]{1,0:T(8,128)} %gram.1.g_ref), custom_call_target="tpu_custom_call" | custom-call | tf_op jit(solution)/shard_map/reduce_all/pallas_call | solution.py:232
  166.3 83.1 %solve.1.c_ref = f32[1024,2048]{1,0:T(8,128)} custom-call(f32[4608,128]{1,0:T(8,128)} %reduce_all.1.g_ref, f32[1024,2048]{1,0:T(8,128)} %get-tuple-element.7.c_ref), custom_call_target="tpu_custom_call" | custom-call | tf_op jit(solution)/shard_map/solve/pallas_call | solution.py:294
  249.4 0.0 copy-start
  249.4 97.7 %collect.1.b_ref = f32[64,32768]{1,0:T(8,128)} custom-call(f32[1024,2048]{1,0:T(8,128)} %solve.1.c_ref), custom_call_target="tpu_custom_call" | custom-call | tf_op jit(solution)/shard_map/collect/pallas_call | solution.py:511
  347.1 0.0 copy-done
  347.1 0.6 broadcast_in_dim.3.grp_ref
  347.7 15.8 %tail.1 = (f32[8,128]{1,0:T(8,128)}, f32[16,128]{1,0:T(8,128)}) custom-call(f32[64,32768]{1,0:T(8,128)} %collect.1.b_ref, f32[64,32768]{1,0:T(8,128)} %get-tuple-element.8.t_ref, s32[8,128]{1,0:T(8,128)} %broadcast_in_dim.3.grp_ref), custom_call_target="tpu_custom_call" | custom-call | tf_op jit(solution)/shard_map/tail/pallas_call | solution.py:689
  363.5 1.2 slice_bitcast_fusion
  364.7 1.3 slice_reduce_fusion
  366.0 7.4 %copy.8 = f32[64,32768]{1,0:T(8,128)} copy(f32[64,32768]{1,0:T(8,128)} %collect.1.b_ref) | data formatting | bytes 16777216
  (1 shorter events, 0.0 us)
Async XLA Ops:
  249.4 97.7 %copy-start = (s32[64]{0:T(128)S(1)}, s32[64]{0:T(128)}, u32[]{:S(2)}) copy-start(s32[64]{0:T(128)} %param.7) | copy-start | bytes 772

commit v4 on v3

--- a/solution.py
+++ b/solution.py
@@ -7,7 +7,7 @@
 from jax.sharding import PartitionSpec as P
 
 BLK = 128
-PAN = 8
+PAN = 16
 F32 = jnp.float32
 BF = jnp.bfloat16
 
@@ -75,11 +75,18 @@
         an = a_ref[pl.ds(nxt, PAN), :]
         xn = an - rows_sum([lanes_of(an, base + m) for m in range(PAN)], xb)
         new_cols = [lanes_of(xn, nxt + m) for m in range(PAN)]
-        for s in range(0, BLK, PAN):
-            a = a_ref[s : s + PAN, :]
-            am = [lanes_of(a, base + m) for m in range(PAN)]
-            a_ref[s : s + PAN, :] = a - rows_sum(am, xb)
-            w_ref[s : s + PAN, :] = w_ref[s : s + PAN, :] - rows_sum(am, kb)
+        raw = carry[0]
+        rh, rm = split(raw)
+        rl = (raw - rh.astype(F32) - rm.astype(F32)).astype(BF)
+        bb = jnp.concatenate([x, kw], axis=1)
+        bh, bm = split(bb)
+        bl = (bb - bh.astype(F32) - bm.astype(F32)).astype(BF)
+        f32 = lambda v: v.astype(F32)
+        left = jnp.concatenate([f32(v) for v in (rh, rh, rm, rm, rh, rl)], axis=0).astype(BF)
+        right = jnp.concatenate([f32(v) for v in (bh, bm, bh, bm, bl, bh)], axis=0).astype(BF)
+        upd = lax.dot_general(left, right, (((0,), (0,)), ((), ())), preferred_element_type=F32)
+        a_ref[...] = a_ref[...] - upd[:, :BLK]
+        w_ref[...] = w_ref[...] - upd[:, BLK:]
         return (xn, *new_cols)
 
     x0 = a_ref[0:PAN, :]
@@ -350,7 +357,7 @@
 HR = 32
 
 
-def ring_kernel(to_rows, side, c_ref, o_ref, src_ref, land_ref, b1_ref, r1_ref, r2_ref,
+def ring_kernel(to_rows, greet, side, done, c_ref, o_ref, src_ref, land_ref, b1_ref, r1_ref, r2_ref,
                 lsem, osem, s1, v1, sr1, vr1, sf1, s2, v2, sr2, vr2, sf2, qsem):
     band, coef, pos = place()
     part = 2048
@@ -386,11 +393,13 @@
     order += [k for k in loads if k not in order and k != (0, 0)] + [(0, 0)]
     for k in order:
         loads[k].start()
+    peers = greet(band, coef) if greet else [
+        (who(h, s, 0), coef) for h in range(2) for s in (1, -1)
+    ]
     barrier = pltpu.get_barrier_semaphore()
-    near_by = [(h, s) for h in range(2) for s in (1, -1)]
-    for h, s in near_by:
-        pl.semaphore_signal(barrier, inc=1, device_id=(who(h, s, 0), coef), device_id_type=MESH)
-    pl.semaphore_wait(barrier, 4)
+    for p in peers:
+        pl.semaphore_signal(barrier, inc=1, device_id=p, device_id_type=MESH)
+    pl.semaphore_wait(barrier, len(peers))
 
     ready = set()
 
@@ -459,11 +468,13 @@
             for h in range(2):
                 dir1[h, r, q].wait_recv()
                 second(h, r, q)
-    for q in (2, 1, 3, 0):
+        side(2)
+    for n, q in enumerate((2, 3, 1, 0)):
         for h in range(2):
             dir1[h, 2, q].wait_recv()
             second(h, 2, q)
-    side(2)
+        if n % 2:
+            side(3)
     for i in range(2):
         for h in range(2):
             for g in range(2):
@@ -472,19 +483,24 @@
                 at = land_ref.at[cell(h, who(h, -r, -SIGN[g]))]
                 fin[h, r, 2] = go(r2_ref.at[h, g, i], at, sf2.at[h, g, i], v2.at[h, r, 1],
                                   (who(h, 0, SIGN[g]), coef))
+    side(4)
+    for r in range(RING):
+        for h in range(2):
+            b = who(h, -r, 0)
+            done(h, b, src_ref.at[cell(h, band)] if r == 0 else b1_ref.at[h, r - 1, 0])
     for r in (0, 1, 3, 2):
         for q in (1, 3, 2):
             for h in range(2):
                 fin[h, r, q].wait_recv()
                 b = who(h, -r, -q)
+                done(h, b, land_ref.at[cell(h, b)])
                 outs.append(
                     pltpu.make_async_copy(land_ref.at[cell(h, b)], o_ref.at[far(h, b)], osem.at[h, r, q - 1])
                 )
                 outs[-1].start()
-    for c in outs:
-        c.wait()
     for c in sent:
         c.wait_send()
+    return outs
 
 
 RING_SCRATCH = [
@@ -502,123 +518,6 @@
 ]
 
 
-def collect_kernel(c_ref, o_ref, *scratch):
-    ring_kernel(False, lambda n: None, c_ref, o_ref, *scratch)
-
-
-def collect(c):
-    n, w = c.shape
-    return pl.pallas_call(
-        collect_kernel,
-        out_shape=jax.ShapeDtypeStruct((n // 16, w * 16), F32),
-        in_specs=[ANY],
-        out_specs=ANY,
-        scratch_shapes=RING_SCRATCH,
-        compiler_params=pltpu.CompilerParams(
-            collective_id=3, has_side_effects=True, vmem_limit_bytes=60 * 2**20
-        ),
-        name="collect",
-    )(c)
-
-
-CH = 2048
-STOPS = (0, 12, 16)
-
-
-def spread_kernel(inv_ref, c_ref, q_ref, o_ref, t_ref, q_all, rows_ref, got_ref, want_ref, isem, tsem, *scratch):
-    bands, width = q_ref.shape
-    n = width // CH
-    loads = []
-    for s in range(n):
-        cols = pl.ds(s * CH, CH)
-        loads.append(pltpu.make_async_copy(q_ref.at[:, cols], q_all.at[:, cols], isem.at[s]))
-    stores = [
-        pltpu.make_async_copy(want_ref.at[s % 2], t_ref.at[:, pl.ds(s * CH, CH)], tsem.at[s]) for s in range(n)
-    ]
-
-    def gather(s):
-        def body(i, _):
-            at = i * 16
-            for u in range(16):
-                got_ref[pl.ds(at + u, 1), :] = rows_ref[pl.ds(inv_ref[s * CH + at + u], 1), :]
-            return 0
-
-        lax.fori_loop(0, CH // 16, body, 0)
-        if s >= 2:
-            stores[s - 2].wait()
-        want_ref[s % 2] = got_ref[...].T
-        stores[s].start()
-
-    def side(stage):
-        if stage == 0:
-            for c in loads:
-                c.start()
-            for s, c in enumerate(loads):
-                c.wait()
-                rows_ref[s * CH : (s + 1) * CH, :] = q_all[:, s * CH : (s + 1) * CH].T
-        else:
-            for s in range(STOPS[stage - 1], STOPS[stage]):
-                gather(s)
-
-    ring_kernel(True, side, c_ref, o_ref, *scratch)
-    for c in stores[-2:]:
-        c.wait()
-
-
-def spread(inv, c, q):
-    a, b = c.shape
-    n = b // CH
-    return pl.pallas_call(
-        spread_kernel,
-        out_shape=(jax.ShapeDtypeStruct((a * 16, b // 16), F32), jax.ShapeDtypeStruct(q.shape, F32)),
-        in_specs=[pl.BlockSpec(memory_space=pltpu.SMEM), ANY, ANY],
-        out_specs=(ANY, ANY),
-        scratch_shapes=[
-            pltpu.VMEM((a, b), F32),
-            pltpu.VMEM((b, a), F32),
-            pltpu.VMEM((CH, a), F32),
-            pltpu.VMEM((2, a, CH), F32),
-            pltpu.SemaphoreType.DMA((n,)),
-            pltpu.SemaphoreType.DMA((n,)),
-            *RING_SCRATCH,
-        ],
-        compiler_params=pltpu.CompilerParams(
-            collective_id=2, has_side_effects=True, vmem_limit_bytes=60 * 2**20
-        ),
-        name="spread",
-    )(inv, c, q)
-
-
-def invert_kernel(idx_ref, inv_ref):
-    n, w = idx_ref.shape
-    his = n * w // BLK
-    acc = jnp.zeros((his, 2 * BLK), F32)
-    for c in range(n):
-        idx = idx_ref[c : c + 1, :]
-        at = c * w + lax.broadcasted_iota(jnp.int32, (1, w), 1)
-        one = lax.broadcasted_iota(jnp.int32, (his, w), 0) == (idx >> 7)
-        low = lax.broadcasted_iota(jnp.int32, (BLK, w), 0) == (idx & 127)
-        hot = jnp.where(one, 1.0, 0.0).astype(BF)
-        top = jnp.where(low, (at >> 7).astype(F32), 0.0).astype(BF)
-        bot = jnp.where(low, (at & 127).astype(F32), 0.0).astype(BF)
-        both = jnp.concatenate([top, bot], axis=0)
-        acc = acc + lax.dot_general(hot, both, (NT, ((), ())), preferred_element_type=F32)
-    inv_ref[...] = acc[:, :BLK].astype(jnp.int32) * BLK + acc[:, BLK:].astype(jnp.int32)
-
-
-def invert(idx):
-    n = idx.shape[0]
-    out = pl.pallas_call(
-        invert_kernel,
-        out_shape=jax.ShapeDtypeStruct((n // BLK, BLK), jnp.int32),
-        in_specs=[pl.BlockSpec(memory_space=pltpu.VMEM)],
-        out_specs=pl.BlockSpec(memory_space=pltpu.VMEM),
-        compiler_params=pltpu.CompilerParams(vmem_limit_bytes=60 * 2**20),
-        name="invert",
-    )(idx.reshape(16, n // 16))
-    return out.reshape(n)
-
-
 def exchange(slots, index, peers, ssem, rsem):
     here = slots.at[index]
     copies = [send(here, here, ssem.at[r], rsem.at[r], p) for r, p in enumerate(peers)]
@@ -627,41 +526,130 @@
     return copies
 
 
-def tail_kernel(b_ref, t_ref, grp_ref, res_ref, tot_ref,
-                land_ref, want_ref, sq_ref, gr_ref, isem, tsem, s2, r2, s3, r3):
+CH = 2048
+
+
+def spread_kernel(idx_ref, c_ref, o_ref, inv_ref, acc_ref, *scratch):
+    tall_, lanes_ = idx_ref.shape
+    group = 16
+
+    def side(stage):
+        if stage:
+            return
+        acc_ref[...] = jnp.zeros_like(acc_ref)
+        lane = lax.broadcasted_iota(jnp.int32, (BLK, lanes_), 1)
+        his = lax.broadcasted_iota(jnp.int32, (tall_, lanes_), 0)
+        los = lax.broadcasted_iota(jnp.int32, (BLK, lanes_), 0)
+
+        def body(c, _):
+            hots, boths = [], []
+            for u in range(group):
+                row = c * group + u
+                idx = idx_ref[pl.ds(row, 1), :]
+                hots.append(jnp.where(his == (idx >> 7), 1.0, 0.0).astype(BF))
+                low = los == (idx & 127)
+                top = jnp.where(low, jnp.full((BLK, lanes_), row, jnp.int32).astype(F32), 0.0)
+                bot = jnp.where(low, lane.astype(F32), 0.0)
+                boths.append(jnp.concatenate([top, bot], axis=0).astype(BF))
+            acc_ref[...] += lax.dot_general(
+                jnp.concatenate(hots, axis=1),
+                jnp.concatenate(boths, axis=1),
+                (NT, ((), ())),
+                preferred_element_type=F32,
+            )
+            return 0
+
+        lax.fori_loop(0, tall_ // group, body, 0)
+        inv_ref[...] = acc_ref[:, :BLK].astype(jnp.int32) * BLK + acc_ref[:, BLK:].astype(jnp.int32)
+
+    outs = ring_kernel(True, None, side, lambda *a: None, c_ref, o_ref, *scratch)
+    for c in outs:
+        c.wait()
+
+
+def spread(idx, c):
+    a, b = c.shape
+    vm = pl.BlockSpec(memory_space=pltpu.VMEM)
+    return pl.pallas_call(
+        spread_kernel,
+        out_shape=(
+            jax.ShapeDtypeStruct((a * 16, b // 16), F32),
+            jax.ShapeDtypeStruct((b // BLK, BLK), jnp.int32),
+        ),
+        in_specs=[vm, ANY],
+        out_specs=(ANY, vm),
+        scratch_shapes=[pltpu.VMEM((b // BLK, 2 * BLK), F32), *RING_SCRATCH],
+        compiler_params=pltpu.CompilerParams(
+            collective_id=2, has_side_effects=True, vmem_limit_bytes=60 * 2**20
+        ),
+        name="spread",
+    )(idx.reshape(b // BLK, BLK), c)
+
+
+STOPS = (0, 2, 4, 6, 8, 10, 12, 14, 16)
+
+
+def collect_kernel(inv_ref, y_ref, q_ref, grp_ref, o_ref, res_ref, tot_ref,
+                   want_ref, rows_ref, got_ref, acc_ref, sq_ref, gr_ref, isem, s2, r2, s3, r3, *scratch):
     band, coef, _ = place()
-    bands, width = b_ref.shape
-    nband = gr_ref.shape[0]
-    part = width // nband
-    ncoef = sq_ref.shape[0]
+    nband, ncoef = gr_ref.shape[0], sq_ref.shape[0]
+    bands, width = q_ref.shape
+    n = width // CH
     bpeers = [(lax.rem(band + r, nband), coef) for r in range(1, nband)]
     cpeers = [(band, lax.rem(coef + r, ncoef)) for r in range(1, ncoef)]
-    ins = []
-    for s in range(nband):
-        cols = pl.ds(s * part, part)
-        ins.append(
-            (
-                pltpu.make_async_copy(b_ref.at[:, cols], land_ref.at[:, cols], isem.at[s]),
-                pltpu.make_async_copy(t_ref.at[:, cols], want_ref.at[:, cols], tsem.at[s]),
-            )
-        )
-        for c in ins[-1]:
-            c.start()
-    barrier = pltpu.get_barrier_semaphore()
-    for p in bpeers + cpeers:
-        pl.semaphore_signal(barrier, inc=1, device_id=p, device_id_type=MESH)
-    pl.semaphore_wait(barrier, nband + ncoef - 2)
-    acc = jnp.zeros((bands, BLK), F32)
-    for s in range(nband):
-        for c in ins[s]:
-            c.wait()
-        d = land_ref[:, s * part : (s + 1) * part] - want_ref[:, s * part : (s + 1) * part]
-        d = d * d
-        for q in range(0, part, BLK):
-            acc = acc + d[:, q : q + BLK]
+
+    def columns(s):
+        return pl.ds(pl.multiple_of(s * CH, CH), CH)
+
+    def load(s):
+        return pltpu.make_async_copy(q_ref.at[:, columns(s)], want_ref.at[:, columns(s)], isem.at[s])
+
+    def turn(s, _):
+        load(s).wait()
+        rows_ref[columns(s), :] = want_ref[:, columns(s)].T
+        return 0
+
+    def gather(s, _):
+        def body(i, _):
+            at = i * 16
+            for u in range(16):
+                got_ref[pl.ds(at + u, 1), :] = rows_ref[pl.ds(inv_ref[s * CH + at + u], 1), :]
+            return 0
+
+        lax.fori_loop(0, CH // 16, body, 0)
+        want_ref[:, columns(s)] = got_ref[...].T
+        return 0
+
+    calls = []
+
+    def side(stage):
+        if stage == 0:
+            acc_ref[...] = jnp.zeros_like(acc_ref)
+            for s in range(n):
+                load(s).start()
+            lax.fori_loop(0, n, turn, 0)
+            return
+        k = len(calls)
+        calls.append(stage)
+        last = STOPS[k + 1] if stage < 4 else n
+        lax.fori_loop(STOPS[k], last, gather, 0)
+
+    def done(h, b, block):
+        step = 4 * BLK
+
+        def body(i, acc):
+            at = pl.multiple_of(i * step, step)
+            d = block[:, pl.ds(at, step)] - want_ref[pl.ds(h * HR, HR), pl.ds(pl.multiple_of(b * CH + at, step), step)]
+            d = d * d
+            return acc + ((d[:, :BLK] + d[:, BLK : 2 * BLK]) + (d[:, 2 * BLK : 3 * BLK] + d[:, 3 * BLK :]))
+
+        acc_ref[h] = lax.fori_loop(0, CH // step, body, acc_ref[h])
+
+    outs = ring_kernel(False, lambda *a: bpeers + cpeers, side, done, y_ref, o_ref, *scratch)
+
     row = lax.broadcasted_iota(jnp.int32, (bands, BLK), 0)
     lane = lax.broadcasted_iota(jnp.int32, (bands, BLK), 1)
-    total = jnp.sum(acc, axis=1, keepdims=True)
+    total = jnp.sum(jnp.concatenate([acc_ref[0], acc_ref[1]], axis=0), axis=1, keepdims=True)
     line = jnp.sum(jnp.where(row == lane, total, 0.0), axis=0, keepdims=True)
     sq_ref[coef] = jnp.broadcast_to(line, (8, BLK))
     c2 = exchange(sq_ref, coef, cpeers, s2, r2)
@@ -676,51 +664,94 @@
     g = gr_ref[0]
     for q in range(1, nband):
         g = g + gr_ref[q]
-    tot_ref[...] = jnp.broadcast_to(jnp.sum(g, axis=1, keepdims=True), (NGROUPS, BLK)) * (NGROUPS / NB)
+    row = lax.broadcasted_iota(jnp.int32, (NGROUPS, BLK), 0)
+    lane = lax.broadcasted_iota(jnp.int32, (NGROUPS, BLK), 1)
+    g = jnp.sum(g, axis=1, keepdims=True) * (NGROUPS / NB)
+    tot_ref[...] = jnp.broadcast_to(jnp.sum(jnp.where(row == lane, g, 0.0), axis=0, keepdims=True), (8, BLK))
+    for c in outs:
+        c.wait()
     for c in c2 + c3:
         c.wait_send()
 
 
-def tail(b, t, grp):
+def collect(inv, y, q, grp):
+    bands, width = q.shape
     vm = pl.BlockSpec(memory_space=pltpu.VMEM)
-    bands, width = t.shape
-    nband = lax.axis_size("band")
-    ncoef = lax.axis_size("coef")
+    nband, ncoef = lax.axis_size("band"), lax.axis_size("coef")
+    dma = pltpu.SemaphoreType.DMA
     return pl.pallas_call(
-        tail_kernel,
+        collect_kernel,
         out_shape=(
+            jax.ShapeDtypeStruct((bands, width), F32),
             jax.ShapeDtypeStruct((8, BLK), F32),
-            jax.ShapeDtypeStruct((NGROUPS, BLK), F32),
+            jax.ShapeDtypeStruct((8, BLK), F32),
         ),
-        in_specs=[ANY, ANY, vm],
-        out_specs=(vm, vm),
+        in_specs=[pl.BlockSpec(memory_space=pltpu.SMEM), ANY, ANY, vm],
+        out_specs=(ANY, vm, vm),
         scratch_shapes=[
             pltpu.VMEM((bands, width), F32),
-            pltpu.VMEM((bands, width), F32),
+            pltpu.VMEM((width, bands), F32),
+            pltpu.VMEM((CH, bands), F32),
+            pltpu.VMEM((2, HR, BLK), F32),
             pltpu.VMEM((ncoef, 8, BLK), F32),
             pltpu.VMEM((nband, NGROUPS, BLK), F32),
-            pltpu.SemaphoreType.DMA((nband,)),
-            pltpu.SemaphoreType.DMA((nband,)),
-            pltpu.SemaphoreType.DMA((ncoef - 1,)),
-            pltpu.SemaphoreType.DMA((ncoef - 1,)),
-            pltpu.SemaphoreType.DMA((nband - 1,)),
-            pltpu.SemaphoreType.DMA((nband - 1,)),
+            dma((width // CH,)),
+            dma((ncoef - 1,)),
+            dma((ncoef - 1,)),
+            dma((nband - 1,)),
+            dma((nband - 1,)),
+            *RING_SCRATCH,
         ],
         compiler_params=pltpu.CompilerParams(
-            collective_id=1, has_side_effects=True, vmem_limit_bytes=60 * 2**20
+            collective_id=3, has_side_effects=True, vmem_limit_bytes=60 * 2**20
         ),
-        name="tail",
-    )(b, t, grp)
+        name="collect",
+    )(inv.reshape(width), y, q, grp)
+
+
+def finish_kernel(raw_ref, res_ref, tot_ref, o_ref, band_ref, group_ref, buf_ref, isem, osem):
+    n = raw_ref.shape[0] // 8
+    ins = [pltpu.make_async_copy(raw_ref.at[pl.ds(8 * s, 8)], buf_ref.at[s], isem.at[s]) for s in range(n)]
+    outs = [pltpu.make_async_copy(buf_ref.at[s], o_ref.at[pl.ds(8 * s, 8)], osem.at[s]) for s in range(n)]
+    for c in ins:
+        c.start()
+    band_ref[...] = res_ref[0, : band_ref.shape[0]]
+    group_ref[...] = tot_ref[0, : group_ref.shape[0]]
+    for a, b in zip(ins, outs):
+        a.wait()
+        b.start()
+    for c in outs:
+        c.wait()
+
+
+def finish(raw, res, tot):
+    bands, width = raw.shape
+    vm = pl.BlockSpec(memory_space=pltpu.VMEM)
+    return pl.pallas_call(
+        finish_kernel,
+        out_shape=(
+            jax.ShapeDtypeStruct((bands, width), F32),
+            jax.ShapeDtypeStruct((bands,), F32),
+            jax.ShapeDtypeStruct((NGROUPS,), F32),
+        ),
+        in_specs=[ANY, vm, vm],
+        out_specs=(ANY, vm, vm),
+        scratch_shapes=[
+            pltpu.VMEM((bands // 8, 8, width), F32),
+            pltpu.SemaphoreType.DMA((bands // 8,)),
+            pltpu.SemaphoreType.DMA((bands // 8,)),
+        ],
+        compiler_params=pltpu.CompilerParams(vmem_limit_bytes=60 * 2**20),
+        name="finish",
+    )(raw, res, tot)
 
 
 def local(coeffs, ref_block, index_map, band_group):
     bands, _ = coeffs.shape
-    columns, moved = spread(invert(index_map), coeffs, ref_block)
+    columns, inv = spread(index_map, coeffs)
     margin = reduce_all(gram(columns))
-    ortho = collect(solve(margin, columns))
     groups = jnp.broadcast_to(jnp.pad(band_group, (0, BLK - bands), constant_values=-1), (8, BLK))
-    res, tot = tail(ortho, moved, groups)
-    return (ortho, res[0, :bands], tot[:, 0])
+    return finish(*collect(inv, solve(margin, columns), ref_block, groups))
 
 
 def solution(mesh):

time: 380 us -> 320 us (0.84); the launches traced: 374 us -> 320 us
  Pallas kernels: 361 us -> 318 us
  local copies, waits for them, and re-layouts: 12.1 us -> 0.6 us
    pallas_call x1, Pallas kernels: 83.1 us -> 45.2 us  [solve(): pl.pallas_call(solve_kernel, out_shape=jax.ShapeDtypeStruct((n, w), F32),...]
    unnamed x3 -> x2, local copies, waits for them, and re-layouts: 7.39 us -> 0.01 us
    pallas_call x3 -> x2, Pallas kernels: 120 us -> 117 us  [the longest x1 110 us: collect(): pl.pallas_call(collect_kernel, out_shape=(jax.ShapeDtypeStruct((bands, wi...]
where the time goes in v4:
time: 320 us
  Pallas kernels  318 us (99%)
    pallas_call x1, Pallas kernels, collect(): pl.pallas_call(collect_kernel, out_shape=(jax.ShapeDtypeStruct((bands, wi...  110 us
    pallas_call x1, Pallas kernels, spread(): pl.pallas_call(spread_kernel, out_shape=(jax.ShapeDtypeStruct((a * 16, b...  102 us
    pallas_call x1, Pallas kernels, solve(): pl.pallas_call(solve_kernel, out_shape=jax.ShapeDtypeStruct((n, w), F32),...  45.2 us
    pallas_call x1, Pallas kernels, reduce_all(): pl.pallas_call(reduce_kernel, out_shape=jax.ShapeDtypeStruct(g.shape, F32...  35 us
    pallas_call x1, Pallas kernels, gram(): pl.pallas_call(gram_kernel, out_shape=jax.ShapeDtypeStruct((TILES * BLK,...  18.4 us
    pallas_call x1, Pallas kernels, finish(): pl.pallas_call(finish_kernel, out_shape=(jax.ShapeDtypeStruct((bands, wid...  7.62 us

profile of v4, /device:TPU:1, one launch (start us, length us, event | category | flops | bytes accessed | tf_op | source)
XLA Modules:
  0.0 319.5 jit_solution(7185455470451422883)
XLA Ops:
  0.6 102.2 %spread.1 = (f32[1024,2048]{1,0:T(8,128)}, s32[256,128]{1,0:T(8,128)}) custom-call(s32[256,128]{1,0:T(8,128)} %bitcast.2, f32[64,32768]{1,0:T(8,128)} %c_ref.1), custom_call_target="tpu_custom_call" | custom-call | tf_op jit(solution)/shard_map/spread/pallas_call | solution.py:573
  102.9 18.4 %gram.1.g_ref = f32[4608,128]{1,0:T(8,128)} custom-call(f32[1024,2048]{1,0:T(8,128)} %get-tuple-element.9.c_ref), custom_call_target="tpu_custom_call" | custom-call | tf_op jit(solution)/shard_map/gram/pallas_call | solution.py:341
  121.2 35.0 %reduce_all.1.g_ref = f32[4608,128]{1,0:T(8,128)} custom-call(f32[4608,128]{1,0:T(8,128)} %gram.1.g_ref), custom_call_target="tpu_custom_call" | custom-call | tf_op jit(solution)/shard_map/reduce_all/pallas_call | solution.py:239
  156.3 0.0 copy-start
  156.3 45.2 %solve.1.y_ref = f32[1024,2048]{1,0:T(8,128)} custom-call(f32[4608,128]{1,0:T(8,128)} %reduce_all.1.g_ref, f32[1024,2048]{1,0:T(8,128)} %get-tuple-element.9.c_ref), custom_call_target="tpu_custom_call" | custom-call | tf_op jit(solution)/shard_map/solve/pallas_call | solution.py:301
  201.5 0.0 copy-done
  201.5 0.6 broadcast_in_dim.3.grp_ref
  202.1 109.6 %collect.1 = (f32[64,32768]{1,0:T(8,128)}, f32[8,128]{1,0:T(8,128)}, f32[8,128]{1,0:T(8,128)}) custom-call(s32[32768]{0:T(1024)} %bitcast.3, f32[1024,2048]{1,0:T(8,128)} %solve.1.y_ref, f32[64,32768]{1,0:T(8,128)} %q_ref.1, s32[8,128]{1,0:T(8,128)} %broadcast_in_dim.3.grp_ref), custom_call_target="tpu_custom_call" | custom-call | tf_op jit(solution)/shard_map/collect/pallas_call | solution.py:682
  311.7 7.6 %finish.1 = (f32[64,32768]{1,0:T(8,128)}, f32[64]{0:T(128)}, f32[16]{0:T(128)}) custom-call(f32[64,32768]{1,0:T(8,128)} %get-tuple-element.10.raw_ref, f32[8,128]{1,0:T(8,128)} %get-tuple-element.11.res_ref, f32[8,128]{1,0:T(8,128)} %get-tuple-element.12.tot_ref), custom_call_target="tpu_custom_call" | custom-call | tf_op jit(solution)/shard_map/finish/pallas_call | solution.py:730
  (1 shorter events, 0.0 us)
Async XLA Ops:
  156.3 45.2 %copy-start = (s32[64]{0:T(128)S(1)}, s32[64]{0:T(128)}, u32[]{:S(2)}) copy-start(s32[64]{0:T(128)} %param.7) | copy-start | bytes 772

commit v5 on v4

--- a/solution.py
+++ b/solution.py
@@ -41,7 +41,7 @@
     return parts[0]
 
 
-def diag_inverse(a_ref, w_ref, m_ref):
+def diag_inverse(a_ref, w_ref, m_ref, side):
     sub = lax.broadcasted_iota(jnp.int32, (PAN, BLK), 0)
     r_i = lax.broadcasted_iota(jnp.int32, (BLK, BLK), 0)
     c_i = lax.broadcasted_iota(jnp.int32, (BLK, BLK), 1)
@@ -72,6 +72,7 @@
         m_ref[pl.ds(base, PAN), :] = fwd * scale
         xb = [row_of(x, m) for m in range(PAN)]
         kb = [row_of(kw, m) for m in range(PAN)]
+        side(p)
         an = a_ref[pl.ds(nxt, PAN), :]
         xn = an - rows_sum([lanes_of(an, base + m) for m in range(PAN)], xb)
         new_cols = [lanes_of(xn, nxt + m) for m in range(PAN)]
@@ -271,18 +272,24 @@
         if k:
             s = s - dot3(lh_ref[lo:, :lo], ll_ref[lo:, :lo], lh_ref[lo:hi, :lo], ll_ref[lo:hi, :lo], NT)
         a_ref[...] = s[:BLK]
-        diag_inverse(a_ref, w_ref, m_ref)
+        loads[k].wait()
+        wide = c_ref.shape[1] // (BLK // PAN)
+
+        def side(p, lo=lo, hi=hi):
+            if lo:
+                cols = pl.ds(pl.multiple_of(p * wide, wide), wide)
+                z_ref[lo:hi, cols] = z_ref[lo:hi, cols] - dot3(
+                    lh_ref[lo:hi, :lo], ll_ref[lo:hi, :lo], yh_ref[:lo, cols], yl_ref[:lo, cols], NN
+                )
+
+        diag_inverse(a_ref, w_ref, m_ref, side)
         mh, ml = split(m_ref[...])
         if hi < n:
             sh, sl = split(s[BLK:])
             lkh, lkl = split(dot3(sh, sl, mh, ml, NT))
             lh_ref[hi:, lo:hi] = lkh
             ll_ref[hi:, lo:hi] = lkl
-        loads[k].wait()
-        z = z_ref[lo:hi, :]
-        if k:
-            z = z - dot3(lh_ref[lo:hi, :lo], ll_ref[lo:hi, :lo], yh_ref[:lo, :], yl_ref[:lo, :], NN)
-        zh, zl = split(z)
+        zh, zl = split(z_ref[lo:hi, :])
         y = dot3(mh, ml, zh, zl, NN)
         z_ref[lo:hi, :] = y
         rows = pl.ds(lo, BLK)
@@ -317,23 +324,28 @@
 
 def gram_kernel(c_ref, g_ref, x_ref, h_ref, l_ref, sem):
     n = c_ref.shape[0]
-    loads = []
-    for i in range(n // GB):
+    loads = {}
+    for i in reversed(range(n // GB)):
         rows = pl.ds(i * GB, GB)
-        loads.append(pltpu.make_async_copy(c_ref.at[rows], x_ref.at[rows], sem.at[i]))
-        loads[-1].start()
-    for i in range(n // GB):
+        loads[i] = pltpu.make_async_copy(c_ref.at[rows], x_ref.at[rows], sem.at[i])
+        loads[i].start()
+    def ready(i):
+        rows = slice(i * GB, (i + 1) * GB)
+        loads[i].wait()
+        h_ref[rows, :], l_ref[rows, :] = split(x_ref[rows, :])
+
+    last = n // GB - 1
+    ready(last)
+    for i in reversed(range(n // GB)):
         lo, e = i * GB, (i + 1) * GB
-        loads[i].wait()
-        h, l = split(x_ref[lo:e, :])
-        h_ref[lo:e, :] = h
-        l_ref[lo:e, :] = l
-        g = dot3(h, l, h_ref[:e, :], l_ref[:e, :], NT)
-        for bi in range(lo // BLK, e // BLK):
-            for bj in range(bi + 1):
+        if i:
+            ready(i - 1)
+        g = dot3(h_ref[lo:, :], l_ref[lo:, :], h_ref[lo:e, :], l_ref[lo:e, :], NT)
+        for bj in range(lo // BLK, e // BLK):
+            for bi in range(bj, n // BLK):
                 t = tile_row(bi, bj)
-                r = bi * BLK - lo
-                g_ref[t : t + BLK, :] = g[r : r + BLK, bj * BLK : (bj + 1) * BLK]
+                r, q = bi * BLK - lo, bj * BLK - lo
+                g_ref[t : t + BLK, :] = g[r : r + BLK, q : q + BLK]
 
 
 def gram(c):

time: 320 us -> 314 us (0.981)
  Pallas kernels: 318 us -> 312 us
where the time goes in v5:
time: 314 us
  Pallas kernels  312 us (99%)
    pallas_call x1, Pallas kernels, collect(): pl.pallas_call(collect_kernel, out_shape=(jax.ShapeDtypeStruct((bands, wi...  110 us
    pallas_call x1, Pallas kernels, spread(): pl.pallas_call(spread_kernel, out_shape=(jax.ShapeDtypeStruct((a * 16, b...  102 us
    pallas_call x1, Pallas kernels, solve(): pl.pallas_call(solve_kernel, out_shape=jax.ShapeDtypeStruct((n, w), F32),...  42.1 us
    pallas_call x1, Pallas kernels, reduce_all(): pl.pallas_call(reduce_kernel, out_shape=jax.ShapeDtypeStruct(g.shape, F32...  35 us
    pallas_call x1, Pallas kernels, gram(): pl.pallas_call(gram_kernel, out_shape=jax.ShapeDtypeStruct((TILES * BLK,...  15.8 us
    pallas_call x1, Pallas kernels, finish(): pl.pallas_call(finish_kernel, out_shape=(jax.ShapeDtypeStruct((bands, wid...  7.62 us

profile of v5, /device:TPU:1, one launch (start us, length us, event | category | flops | bytes accessed | tf_op | source)
XLA Modules:
  0.0 313.9 jit_solution(14889404443202401612)
XLA Ops:
  0.6 102.2 %spread.1 = (f32[1024,2048]{1,0:T(8,128)}, s32[256,128]{1,0:T(8,128)}) custom-call(s32[256,128]{1,0:T(8,128)} %bitcast.2, f32[64,32768]{1,0:T(8,128)} %c_ref.1), custom_call_target="tpu_custom_call" | custom-call | tf_op jit(solution)/shard_map/spread/pallas_call | solution.py:585
  102.9 15.8 %gram.1.g_ref = f32[4608,128]{1,0:T(8,128)} custom-call(f32[1024,2048]{1,0:T(8,128)} %get-tuple-element.9.c_ref), custom_call_target="tpu_custom_call" | custom-call | tf_op jit(solution)/shard_map/gram/pallas_call | solution.py:353
  118.7 35.0 %reduce_all.1.g_ref = f32[4608,128]{1,0:T(8,128)} custom-call(f32[4608,128]{1,0:T(8,128)} %gram.1.g_ref), custom_call_target="tpu_custom_call" | custom-call | tf_op jit(solution)/shard_map/reduce_all/pallas_call | solution.py:240
  153.7 0.0 copy-start
  153.7 42.1 %solve.1.y_ref = f32[1024,2048]{1,0:T(8,128)} custom-call(f32[4608,128]{1,0:T(8,128)} %reduce_all.1.g_ref, f32[1024,2048]{1,0:T(8,128)} %get-tuple-element.9.c_ref), custom_call_target="tpu_custom_call" | custom-call | tf_op jit(solution)/shard_map/solve/pallas_call | solution.py:308
  195.8 0.0 copy-done
  195.9 0.6 broadcast_in_dim.3.grp_ref
  196.5 109.7 %collect.1 = (f32[64,32768]{1,0:T(8,128)}, f32[8,128]{1,0:T(8,128)}, f32[8,128]{1,0:T(8,128)}) custom-call(s32[32768]{0:T(1024)} %bitcast.3, f32[1024,2048]{1,0:T(8,128)} %solve.1.y_ref, f32[64,32768]{1,0:T(8,128)} %q_ref.1, s32[8,128]{1,0:T(8,128)} %broadcast_in_dim.3.grp_ref), custom_call_target="tpu_custom_call" | custom-call | tf_op jit(solution)/shard_map/collect/pallas_call | solution.py:694
  306.1 7.6 %finish.1 = (f32[64,32768]{1,0:T(8,128)}, f32[64]{0:T(128)}, f32[16]{0:T(128)}) custom-call(f32[64,32768]{1,0:T(8,128)} %get-tuple-element.10.raw_ref, f32[8,128]{1,0:T(8,128)} %get-tuple-element.11.res_ref, f32[8,128]{1,0:T(8,128)} %get-tuple-element.12.tot_ref), custom_call_target="tpu_custom_call" | custom-call | tf_op jit(solution)/shard_map/finish/pallas_call | solution.py:742
  (1 shorter events, 0.0 us)
Async XLA Ops:
  153.7 42.1 %copy-start = (s32[64]{0:T(128)S(1)}, s32[64]{0:T(128)}, u32[]{:S(2)}) copy-start(s32[64]{0:T(128)} %param.7) | copy-start | bytes 772
